TPU v7x, 256 devices: a 4x2x16 block of a 4x16x16 slice. The times are simulated.
256 devices in a mesh: groups: 2 (over y), row: 128 (over x, z, core).
Axes of the slice: x: 4, y: 2, z: 16, core: 2. Of those that a mesh axis runs over, the one named last changes fastest.
The devices are a block of a 4x16x16 slice.
Arguments:
- pair_cols: bfloat16 [1024, 2048, 128], P(None, ('groups', 'row')), parts along dimension 1, may hold values from -410 to 410
- single: bfloat16 [2048, 384], P(('groups', 'row')), parts along dimension 0, may hold values from -6 to 6
- rotation: float32 [9, 2048], P(None, ('groups', 'row')), parts along dimension 1, may hold values from -1 to 1, as said below
- translation: float32 [3, 2048], P(None, ('groups', 'row')), parts along dimension 1, may hold values from -6 to 6
- residue_mask: int32 [2048], P('groups'), parts along dimension 0, may hold values from 0 to 1, as said below
- chain_index: int32 [2048], P('groups'), parts along dimension 0, may hold values from 0 to 3, never falling along the last dimension, each value on 1 to 512 neighbouring positions
- query_weight: bfloat16 [384, 192], replicated, may hold values from -0.3125 to 0.3125
- key_weight: bfloat16 [384, 192], replicated, may hold values from -0.3125 to 0.3125
- value_weight: bfloat16 [384, 192], replicated, may hold values from -0.3125 to 0.3125
- qpoint_weight: bfloat16 [384, 144], replicated, may hold values from -0.3125 to 0.3125
- kpoint_weight: bfloat16 [384, 144], replicated, may hold values from -0.3125 to 0.3125
- vpoint_weight: bfloat16 [384, 288], replicated, may hold values from -0.3125 to 0.3125
- pair_weight: bfloat16 [12, 128], replicated, may hold values from -0.5 to 0.5
- head_weight: float32 [12], replicated, may hold values from -3 to 3
- chain_weight: float32 [12], replicated, may hold values from -6 to 6
- output_weight: bfloat16 [2112, 384], replicated, may hold values from -0.125 to 0.125
- gain_first: float32 [384], replicated, may hold values from 0.5 to 1.5
- mlp_first: bfloat16 [384, 384], replicated, may hold values from -0.3125 to 0.3125
- mlp_second: bfloat16 [384, 384], replicated, may hold values from -0.3125 to 0.3125
- mlp_third: bfloat16 [384, 384], replicated, may hold values from -0.3125 to 0.3125
- gain_second: float32 [384], replicated, may hold values from 0.5 to 1.5
- frame_weight: bfloat16 [384, 6], replicated, may hold values from -0.3125 to 0.3125
Outputs:
- single_out: float32 [2048, 384], P(('groups', 'row')), parts along dimension 0
- rotation_out: float32 [9, 2048], P(None, ('groups', 'row')), parts along dimension 1
- translation_out: float32 [3, 2048], P(None, ('groups', 'row')), parts along dimension 1
There are 2 independent parts, one for each index of `groups`. A program takes and returns all parts, laid end to end along the dimension named above; an argument that names none is the same for every part. Nothing has to cross between parts.
Inputs may be any that keep to these rules, and one draw needn't show every extreme that they name: `residue_mask`: 1 on a leading run of at least three quarters of 1024 positions, 0 after it. Each column is a rotation matrix, row-major.
All inputs are finite; a program needn't handle non-finite values.
Results may differ from a plain program's by a relative error of at most 0.02.
Values may be sent and summed in bfloat16 or wider, within the bound.
A program may use at most 64 MiB of HBM per device.

v0:
```python
import jax
import jax.numpy as jnp
from jax import lax
from jax.sharding import Mesh
from jax.sharding import PartitionSpec as P

LAYERS = 2
ROW = ("row_0", "row_1", "row_2")
GROUPS_ROW = ("groups", "row_0", "row_1", "row_2")


EXACT_PRODUCT = lax.Precision.HIGHEST
LOGIT_WEIGHT = (1.0 / 3.0) ** 0.5


def grouped_exchange(array, axis, split_dim, concat_dim, work, item_dim, out_dim):
    items = jax.tree.leaves(array)[0].shape[item_dim]
    count = 2 if items % 2 == 0 else 1
    done = []
    for k in range(count):
        group = jax.tree.map(
            lambda a: lax.slice_in_dim(
                a, k * (items // count), (k + 1) * (items // count), axis=item_dim
            ),
            array,
        )
        done.append(
            work(
                lax.all_to_all(
                    group, axis, split_axis=split_dim, concat_axis=concat_dim, tiled=True
                )
            )
        )
    return jax.tree.map(lambda *parts: jnp.concatenate(parts, axis=out_dim), *done)


def laid_out(pieces, dim):
    pieces = jnp.moveaxis(pieces, 0, dim)
    dims = pieces.shape
    return pieces.reshape(*dims[:dim], dims[dim] * dims[dim + 1], *dims[dim + 2 :])


def all_blocks(array, axes, turns):
    pieces = array[None]
    for k in turns:
        pieces = lax.all_gather(pieces, axes[k], axis=0, tiled=True)
    held = [lax.axis_size(axes[k]) for k in reversed(turns)]
    pieces = pieces.reshape(*held, *array.shape)
    turned = sorted(range(len(turns)), key=lambda place: turns[len(turns) - 1 - place])
    return pieces.transpose(*turned, *range(len(turns), pieces.ndim)).reshape(-1, *array.shape)


def gather_axes(array, axes, turns, dim):
    return laid_out(all_blocks(array, axes, turns), dim)


def to_global(points, rotation, translation):
    components = []
    for component in range(3):
        components.append(
            rotation[3 * component][:, None] * points[:, 0]
            + rotation[3 * component + 1][:, None] * points[:, 1]
            + rotation[3 * component + 2][:, None] * points[:, 2]
            + translation[component][:, None]
        )
    return jnp.stack(components, axis=1)


def to_local(points, rotation, translation):
    shifted = points - jnp.transpose(translation)[:, :, None]
    components = []
    for component in range(3):
        components.append(
            rotation[component][:, None] * shifted[:, 0]
            + rotation[3 + component][:, None] * shifted[:, 1]
            + rotation[6 + component][:, None] * shifted[:, 2]
        )
    return jnp.stack(components, axis=1)


def layer_norm(values, gain_vector):
    centered = values - jnp.mean(values, axis=-1, keepdims=True)
    variance = jnp.mean(centered * centered, axis=-1, keepdims=True)
    return centered * lax.rsqrt(variance + 1e-05) * gain_vector


def project_bias(pair_rows, pair_weight):
    return jnp.einsum("ijc,hc->ihj", pair_rows, pair_weight, preferred_element_type=jnp.float32)


def key_side(
    state_bf, rotation, translation, key_weight, value_weight, kpoint_weight, vpoint_weight
):
    key_count = state_bf.shape[0]
    keys_bf = jnp.dot(state_bf, key_weight, preferred_element_type=jnp.float32).astype(jnp.bfloat16)
    values_bf = jnp.dot(state_bf, value_weight, preferred_element_type=jnp.float32).astype(
        jnp.bfloat16
    )
    key_pts = jnp.dot(state_bf, kpoint_weight, preferred_element_type=jnp.float32).reshape(
        key_count, 3, -1
    )
    value_pts = jnp.dot(state_bf, vpoint_weight, preferred_element_type=jnp.float32).reshape(
        key_count, 3, -1
    )
    return (
        keys_bf,
        values_bf,
        to_global(key_pts, rotation, translation),
        to_global(value_pts, rotation, translation),
    )


def attend(
    state_bf,
    rotation,
    translation,
    pair_rows,
    pair_bias,
    chain_rows,
    keys_bf,
    values_bf,
    key_global,
    value_global,
    chain_index,
    residue_mask,
    query_weight,
    qpoint_weight,
    head_weight,
    chain_weight,
):
    row_count = state_bf.shape[0]
    heads = head_weight.shape[0]
    key_count = keys_bf.shape[0]
    queries = (
        jnp.dot(state_bf, query_weight, preferred_element_type=jnp.float32)
        .astype(jnp.bfloat16)
        .reshape(row_count, heads, -1)
    )
    head_dim = queries.shape[2]
    query_pts = to_global(
        jnp.dot(state_bf, qpoint_weight, preferred_element_type=jnp.float32).reshape(
            row_count, 3, -1
        ),
        rotation,
        translation,
    )
    query_pts = query_pts.reshape(row_count, 3, heads, -1)
    key_pts = key_global.reshape(key_count, 3, heads, -1)
    point_count = query_pts.shape[3]
    scores = jnp.einsum(
        "ihd,jhd->ihj",
        queries,
        keys_bf.reshape(key_count, heads, head_dim),
        preferred_element_type=jnp.float32,
    )
    cross_term = jnp.einsum("ikhp,jkhp->ihj", query_pts, key_pts, precision=EXACT_PRODUCT)
    query_square = jnp.sum(query_pts * query_pts, axis=(1, 3))
    key_square = jnp.sum(key_pts * key_pts, axis=(1, 3))
    distance = query_square[:, :, None] + jnp.transpose(key_square)[None] - 2.0 * cross_term
    weight_c = (2.0 / (9.0 * point_count)) ** 0.5
    point_scale = jax.nn.softplus(head_weight)
    same_chain = (chain_rows[:, None] == chain_index[None, :]).astype(jnp.float32)
    logits = LOGIT_WEIGHT * (
        scores * head_dim ** (-0.5)
        + pair_bias
        - (0.5 * weight_c * point_scale)[None, :, None] * distance
    )
    logits = (
        logits
        + chain_weight[None, :, None] * same_chain[:, None, :]
        + ((residue_mask.astype(jnp.float32) - 1.0) * 100000.0)[None, None, :]
    )
    attention = jax.nn.softmax(logits, axis=-1).astype(jnp.bfloat16)
    outputs = jnp.einsum(
        "ihj,jhd->ihd",
        attention,
        values_bf.reshape(key_count, heads, head_dim),
        preferred_element_type=jnp.float32,
    )
    value_pts = value_global.reshape(key_count, 3, heads, -1)
    point_glob = jnp.einsum(
        "ihj,jkhp->ikhp", attention.astype(jnp.float32), value_pts, precision=EXACT_PRODUCT
    )
    point_local = to_local(point_glob.reshape(row_count, 3, -1), rotation, translation)
    point_norms = jnp.sqrt(jnp.sum(point_local * point_local, axis=1) + 1e-08)
    pair_out = jnp.einsum("ihj,ijc->ihc", attention, pair_rows, preferred_element_type=jnp.float32)
    return jnp.concatenate(
        [
            outputs.reshape(row_count, -1),
            point_local.reshape(row_count, -1),
            point_norms,
            pair_out.reshape(row_count, -1),
        ],
        axis=1,
    ).astype(jnp.bfloat16)


def frame_compose(rotation, translation, frame_update):
    inverse = lax.rsqrt(1.0 + jnp.sum(frame_update[:, :3] * frame_update[:, :3], axis=1))
    vector_x = frame_update[:, 0] * inverse
    vector_y = frame_update[:, 1] * inverse
    vector_z = frame_update[:, 2] * inverse
    turn_matrix = [
        [
            inverse * inverse + vector_x * vector_x - vector_y * vector_y - vector_z * vector_z,
            2.0 * (vector_x * vector_y - inverse * vector_z),
            2.0 * (vector_x * vector_z + inverse * vector_y),
        ],
        [
            2.0 * (vector_x * vector_y + inverse * vector_z),
            inverse * inverse - vector_x * vector_x + vector_y * vector_y - vector_z * vector_z,
            2.0 * (vector_y * vector_z - inverse * vector_x),
        ],
        [
            2.0 * (vector_x * vector_z - inverse * vector_y),
            2.0 * (vector_y * vector_z + inverse * vector_x),
            inverse * inverse - vector_x * vector_x - vector_y * vector_y + vector_z * vector_z,
        ],
    ]
    new_rotation = jnp.stack(
        [
            rotation[3 * outer] * turn_matrix[0][inner]
            + rotation[3 * outer + 1] * turn_matrix[1][inner]
            + rotation[3 * outer + 2] * turn_matrix[2][inner]
            for outer in range(3)
            for inner in range(3)
        ]
    )
    new_translation = jnp.stack(
        [
            rotation[3 * outer] * frame_update[:, 3]
            + rotation[3 * outer + 1] * frame_update[:, 4]
            + rotation[3 * outer + 2] * frame_update[:, 5]
            + translation[outer]
            for outer in range(3)
        ]
    )
    return (new_rotation, new_translation)


def update(
    single_state,
    concat,
    rotation,
    translation,
    output_weight,
    gain_first,
    mlp_first,
    mlp_second,
    mlp_third,
    gain_second,
    frame_weight,
):
    single_state = single_state + jnp.dot(concat, output_weight, preferred_element_type=jnp.float32)
    normed = layer_norm(single_state, gain_first)
    hidden = jax.nn.relu(
        jnp.dot(normed.astype(jnp.bfloat16), mlp_first, preferred_element_type=jnp.float32)
    ).astype(jnp.bfloat16)
    hidden = jax.nn.relu(jnp.dot(hidden, mlp_second, preferred_element_type=jnp.float32)).astype(
        jnp.bfloat16
    )
    single_state = layer_norm(
        normed + jnp.dot(hidden, mlp_third, preferred_element_type=jnp.float32), gain_second
    )
    state_bf = single_state.astype(jnp.bfloat16)
    frame_update = jnp.dot(state_bf, frame_weight, preferred_element_type=jnp.float32)
    new_rotation, new_translation = frame_compose(rotation, translation, frame_update)
    return (single_state, state_bf, new_rotation, new_translation)


def on_device(
    pair_cols,
    single,
    rotation,
    translation,
    residue_mask,
    chain_index,
    query_weight,
    key_weight,
    value_weight,
    qpoint_weight,
    kpoint_weight,
    vpoint_weight,
    pair_weight,
    head_weight,
    chain_weight,
    output_weight,
    gain_first,
    mlp_first,
    mlp_second,
    mlp_third,
    gain_second,
    frame_weight,
):
    axis_size = lax.axis_size(ROW)
    row_count = single.shape[0]
    row_start = lax.axis_index(ROW) * row_count
    blocks = pair_cols.reshape(axis_size, row_count, pair_cols.shape[1], pair_cols.shape[2])

    def project_rows(piece_rows):
        arrived = piece_rows[0]
        return (arrived, project_bias(arrived, pair_weight))

    pair_rows, pair_bias = grouped_exchange(blocks, ROW, 0, 2, project_rows, 1, 0)
    chain_rows = lax.dynamic_slice_in_dim(chain_index, row_start, row_count)
    single_state = single.astype(jnp.float32)
    state_bf = single
    channels = single.shape[1]
    for layer_index in range(LAYERS):
        packed = jnp.concatenate(
            [state_bf.astype(jnp.float32), jnp.transpose(rotation), jnp.transpose(translation)],
            axis=1,
        )
        gathered = gather_axes(packed, ROW, (0, 1, 2), 0)
        single_all = gathered[:, :channels].astype(jnp.bfloat16)
        rotation_all = jnp.transpose(gathered[:, channels : channels + 9])
        translation_all = jnp.transpose(gathered[:, channels + 9 : channels + 12])
        keys_bf, values_bf, key_global, value_global = key_side(
            single_all,
            rotation_all,
            translation_all,
            key_weight,
            value_weight,
            kpoint_weight,
            vpoint_weight,
        )
        concat = attend(
            state_bf,
            rotation,
            translation,
            pair_rows,
            pair_bias,
            chain_rows,
            keys_bf,
            values_bf,
            key_global,
            value_global,
            chain_index,
            residue_mask,
            query_weight,
            qpoint_weight,
            head_weight,
            chain_weight,
        )
        single_state, state_bf, rotation, translation = update(
            single_state,
            concat,
            rotation,
            translation,
            output_weight,
            gain_first,
            mlp_first,
            mlp_second,
            mlp_third,
            gain_second,
            frame_weight,
        )
    return (single_state, rotation, translation)


def solution(mesh):
    finer = Mesh(
        mesh.devices.reshape(mesh.shape["groups"], 4, 16, 2), ("groups", "row_0", "row_1", "row_2")
    )
    in_specs = (
        P(None, GROUPS_ROW, None),
        P(GROUPS_ROW, None),
        P(None, GROUPS_ROW),
        P(None, GROUPS_ROW),
        P("groups"),
        P("groups"),
        P(),
        P(),
        P(),
        P(),
        P(),
        P(),
        P(),
        P(),
        P(),
        P(),
        P(),
        P(),
        P(),
        P(),
        P(),
        P(),
    )
    out_specs = (P(GROUPS_ROW, None), P(None, GROUPS_ROW), P(None, GROUPS_ROW))
    return jax.shard_map(
        on_device, mesh=finer, in_specs=in_specs, out_specs=out_specs, check_vma=False
    )
```

profile of v0, /device:TPU:33, one launch (start us, length us, event | category | flops | bytes accessed | tf_op | source)
XLA Modules:
  0.0 307.3 jit_solution(4317316415544409495)
XLA Ops:
  7.2 3.4 %fusion.139 = (bf16[128,4,8,128]{3,2,1,0:T(8,128)(2,1)}, bf16[128,4,8,128]{3,2,1,0:T(8,128)(2,1)}) fusion(bf16[128,8,8,128]{3,2,1,0:T(8,128)(2,1)} %bitcast.587), kind=kLoop, calls=%fused_computation.381 | loop fusion | bytes 4194304 | tf_op jit(solution)/shard_map/slice | solution.py:22
  10.6 31.1 %all-to-all-start.1 = ((bf16[128,4,8,128]{3,2,1,0:T(8,128)(2,1)}), bf16[128,4,8,128]{3,2,1,0:T(8,128)(2,1)S(1)}, u32[]{:S(2)}, u32[]{:S(2)}) async-start(bf16[128,4,8,128]{3,2,1,0:T(8,128)(2,1)} %get-tuple-element.96), calls=%async_computation.1 | async-start | bytes 2097152 | tf_op jit(solution)/shard_map/all_to_all | solution.py:29
  42.0 11.5 %all-gather = f32[32,396]{1,0:T(8,128)S(1)} all-gather(f32[8,396]{1,0:T(8,128)S(1)} %pad_maximum_fusion.16), channel_id=2, replica_groups=mesh['groups'=2,'row_0'=4,'row_1'=16,'row_2'=2] {'row_0'}, dimensions={0}, use_global_device_ids=true | all-gather | bytes 63360 | tf_op jit(solution)/shard_map/all_gather | solution.py:46
  53.5 60.2 %all_gather.19 = f32[64,8,396]{2,1,0:T(8,128)} all-gather(f32[4,8,396]{2,1,0:T(8,128)S(1)} %bitcast.598), channel_id=1, replica_groups=mesh['groups'=2,'row_0'=4,'row_1'=16,'row_2'=2] {'row_1'}, dimensions={0}, use_global_device_ids=true | all-gather | bytes 861696 | tf_op jit(solution)/shard_map/all_gather | solution.py:46
  115.4 23.6 %all-to-all-start = ((bf16[128,4,8,128]{3,2,1,0:T(8,128)(2,1)}), bf16[128,4,8,128]{3,2,1,0:T(8,128)(2,1)}, u32[]{:S(2)}, u32[]{:S(2)}) async-start(bf16[128,4,8,128]{3,2,1,0:T(8,128)(2,1)} %get-tuple-element.95), calls=%async_computation | async-start | bytes 2097152 | tf_op jit(solution)/shard_map/all_to_all | solution.py:29
  139.8 0.7 copy.385
  140.7 0.7 reshape.1505
  142.1 0.7 compare_convert_fusion
  142.7 1.8 copy.365
  145.0 3.2 %slice_reduce_fusion.12 = (f32[1024]{0:T(1024)S(1)}, f32[1024]{0:T(1024)S(1)}, f32[1024]{0:T(1024)S(1)}, f32[1024]{0:T(1024)S(1)}, f32[1024]{0:T(1024)S(1)}, /*i...) fusion(f32[3,1024]{0,1:T(8,128)S(1)} %slice_bitcast_fusion.2, ...), kind=kLoop, calls=%fused_computation.93 | loop fusion | bytes 98304 | tf_op jit(solution)/shard_map/slice | solution.py:64
  148.8 0.8 add_add_fusion.3
  149.7 1.7 stack.124
  151.4 1.4 add_add_fusion.4
  152.8 1.0 stack.125
  153.8 1.0 stack.126
  154.8 0.9 constant_dynamic-update-slice_fusion.2
  156.1 1.9 fusion.156
  158.2 0.9 add_bitcast_fusion.3
  159.1 1.6 fusion.23
  160.7 1.1 add_bitcast_fusion.5
  162.2 1.2 convolution_convert_fusion.2
  163.8 27.9 %all-to-all-done = bf16[128,4,8,128]{3,2,1,0:T(8,128)(2,1)} async-done(((bf16[128,4,8,128]{3,2,1,0:T(8,128)(2,1)}), bf16[128,4,8,128]{3,2,1,0:T(8,128)(2,1)}, u32[]{:S(2)}, u32[]{:S(2)}) %all-to-all-start) | async-done | bytes 1048608 | tf_op jit(solution)/shard_map/all_to_all | solution.py:29
  191.7 1.6 fusion.89
  193.3 1.0 copy_bitcast_fusion.2
  194.5 2.4 fusion.142
  196.9 1.1 divide_convert_fusion.1
  198.0 0.7 copy-done.7
  198.6 2.6 fusion.43
  201.2 1.0 copy.384
  202.7 1.2 fusion.50
  204.3 1.8 copy_bitcast_fusion.1
  211.4 9.9 %all-gather.1 = f32[32,396]{1,0:T(8,128)S(1)} all-gather(f32[8,396]{1,0:T(8,128)S(1)} %pad_maximum_fusion.17), channel_id=3, replica_groups=mesh['groups'=2,'row_0'=4,'row_1'=16,'row_2'=2] {'row_0'}, dimensions={0}, use_global_device_ids=true | all-gather | bytes 63360 | tf_op jit(solution)/shard_map/all_gather | solution.py:46
  221.3 29.4 %all_gather.22 = f32[64,8,396]{2,1,0:T(8,128)} all-gather(f32[4,8,396]{2,1,0:T(8,128)S(1)} %bitcast.599), channel_id=1, replica_groups=mesh['groups'=2,'row_0'=4,'row_1'=16,'row_2'=2] {'row_1'}, dimensions={0}, use_global_device_ids=true | all-gather | bytes 861696 | tf_op jit(solution)/shard_map/all_gather | solution.py:46
  250.8 0.7 copy.421
  252.6 0.7 reshape.1517
  254.0 22.5 %all-gather.7.cloned.1.call-done = f32[128,8,396]{2,1,0:T(8,128)} async-done(((f32[64,8,396]{2,1,0:T(8,128)}), f32[128,8,396]{2,1,0:T(8,128)}) %all-gather.7.cloned.1.call-update) | async-done | bytes 1622032 | tf_op jit(solution)/shard_map/all_gather | solution.py:46
  276.5 1.8 copy.408
  280.3 1.2 convolution_convert_fusion
  282.0 0.8 slice_reduce_fusion
  282.7 2.4 slice_reduce_fusion.3
  285.1 0.9 add_bitcast_fusion
  286.2 1.1 add_bitcast_fusion.2
  287.8 1.6 fusion.27
  289.5 1.6 fusion.145
  291.2 2.0 fusion.40
  293.7 2.1 fusion.48
  299.1 0.7 copy.444
  299.8 0.7 stack.148
  (429 shorter events, 19.5 us)
Async XLA Ops:
  7.2 200.0 %copy-start = (bf16[2112,384]{1,0:T(8,128)(2,1)S(1)}, bf16[2112,384]{1,0:T(8,128)(2,1)}, u32[]{:S(2)}) copy-start(bf16[2112,384]{1,0:T(8,128)(2,1)} %param.37) | copy-start | bytes 4866052
  10.6 31.3 %copy-start.137 = (f32[3,8]{1,0:T(4,128)S(1)}, f32[3,8]{1,0:T(4,128)}, u32[]{:S(2)}) copy-start(f32[3,8]{1,0:T(4,128)} %param.25) | copy-start | bytes 292
  10.6 31.4 %copy-start.30 = (bf16[8,384]{1,0:T(8,128)(2,1)S(1)}, bf16[8,384]{1,0:T(8,128)(2,1)}, u32[]{:S(2)}) copy-start(bf16[8,384]{1,0:T(8,128)(2,1)} %param.23) | copy-start | bytes 18436
  10.6 31.4 %copy-start.3 = (f32[9,8]{0,1:T(8,128)S(1)}, f32[9,8]{0,1:T(8,128)}, u32[]{:S(2)}) copy-start(f32[9,8]{0,1:T(8,128)} %param.24) | copy-start | bytes 868
  10.6 103.2 %copy-start.15 = (bf16[384,144]{0,1:T(8,128)(2,1)S(1)}, bf16[384,144]{0,1:T(8,128)(2,1)}, u32[]{:S(2)}) copy-start(bf16[384,144]{0,1:T(8,128)(2,1)} %param.31) | copy-start | bytes 331780
  10.6 103.8 %copy-start.132 = (s32[1024]{0:T(1024)S(1)}, s32[1024]{0:T(1024)}, u32[]{:S(2)}) copy-start(s32[1024]{0:T(1024)} %param.26) | copy-start | bytes 12292
  10.6 104.6 %copy-start.13 = (bf16[384,192]{0,1:T(8,128)(2,1)S(1)}, bf16[384,192]{0,1:T(8,128)(2,1)}, u32[]{:S(2)}) copy-start(bf16[384,192]{0,1:T(8,128)(2,1)} %param.28) | copy-start | bytes 442372
  10.6 104.8 %all-to-all-start.1 = ((bf16[128,4,8,128]{3,2,1,0:T(8,128)(2,1)}), bf16[128,4,8,128]{3,2,1,0:T(8,128)(2,1)S(1)}, u32[]{:S(2)}, u32[]{:S(2)}) async-start(bf16[128,4,8,128]{3,2,1,0:T(8,128)(2,1)} %get-tuple-element.96), calls=%async_computation.1 | async-start | bytes 2097152 | tf_op jit(solution)/shard_map/all_to_all | solution.py:29
  41.8 101.0 %all-gather.5.cloned.1.call-start = ((), (), s32[]{:S(2)}) async-start(), calls=%async_computation.2 | async-start | bytes 3145728 | tf_op jit(solution)/shard_map/all_gather | solution.py:46
  53.5 85.7 %copy-start.146 = (f32[12]{0:T(128)S(1)}, f32[12]{0:T(128)}, u32[]{:S(2)}) copy-start(f32[12]{0:T(128)} %param.35) | copy-start | bytes 148
  113.7 27.6 %copy-start.131 = (s32[1024]{0:T(1024)S(1)}, s32[1024]{0:T(1024)}, u32[]{:S(2)}) copy-start(s32[1024]{0:T(1024)} %param.27) | copy-start | bytes 12292
  114.4 30.2 %copy-start.85 = (f32[8]{0:T(128)}, f32[8]{0:T(128)S(1)}, u32[]{:S(2)}) copy-start(f32[8]{0:T(128)S(1)} %get-tuple-element.221) | copy-start | bytes 100
  114.4 30.2 %copy-start.87 = (f32[8]{0:T(128)}, f32[8]{0:T(128)S(1)}, u32[]{:S(2)}) copy-start(f32[8]{0:T(128)S(1)} %get-tuple-element.222) | copy-start | bytes 100
  114.4 30.2 %copy-start.89 = (f32[8]{0:T(128)}, f32[8]{0:T(128)S(1)}, u32[]{:S(2)}) copy-start(f32[8]{0:T(128)S(1)} %get-tuple-element.225) | copy-start | bytes 100
  114.4 30.2 %copy-start.91 = (f32[8]{0:T(128)}, f32[8]{0:T(128)S(1)}, u32[]{:S(2)}) copy-start(f32[8]{0:T(128)S(1)} %get-tuple-element.226) | copy-start | bytes 100
  114.4 30.2 %copy-start.93 = (f32[8]{0:T(128)}, f32[8]{0:T(128)S(1)}, u32[]{:S(2)}) copy-start(f32[8]{0:T(128)S(1)} %get-tuple-element.227) | copy-start | bytes 100
  114.5 30.2 %copy-start.95 = (f32[8]{0:T(128)}, f32[8]{0:T(128)S(1)}, u32[]{:S(2)}) copy-start(f32[8]{0:T(128)S(1)} %get-tuple-element.228) | copy-start | bytes 100
  114.5 30.2 %copy-start.97 = (f32[8]{0:T(128)}, f32[8]{0:T(128)S(1)}, u32[]{:S(2)}) copy-start(f32[8]{0:T(128)S(1)} %get-tuple-element.223) | copy-start | bytes 100
  114.5 30.2 %copy-start.99 = (f32[8]{0:T(128)}, f32[8]{0:T(128)S(1)}, u32[]{:S(2)}) copy-start(f32[8]{0:T(128)S(1)} %get-tuple-element.224) | copy-start | bytes 100
  114.5 30.2 %copy-start.101 = (f32[8]{0:T(128)}, f32[8]{0:T(128)S(1)}, u32[]{:S(2)}) copy-start(f32[8]{0:T(128)S(1)} %get-tuple-element.229) | copy-start | bytes 100
  114.5 30.2 %copy-start.105 = (f32[8]{0:T(128)}, f32[8]{0:T(128)S(1)}, u32[]{:S(2)}) copy-start(f32[8]{0:T(128)S(1)} %get-tuple-element.54) | copy-start | bytes 100
  114.5 30.2 %copy-start.107 = (f32[8]{0:T(128)}, f32[8]{0:T(128)S(1)}, u32[]{:S(2)}) copy-start(f32[8]{0:T(128)S(1)} %get-tuple-element.55) | copy-start | bytes 100
  114.5 30.2 %copy-start.109 = (f32[8]{0:T(128)}, f32[8]{0:T(128)S(1)}, u32[]{:S(2)}) copy-start(f32[8]{0:T(128)S(1)} %get-tuple-element.56) | copy-start | bytes 100
  115.4 76.4 %all-to-all-start = ((bf16[128,4,8,128]{3,2,1,0:T(8,128)(2,1)}), bf16[128,4,8,128]{3,2,1,0:T(8,128)(2,1)}, u32[]{:S(2)}, u32[]{:S(2)}) async-start(bf16[128,4,8,128]{3,2,1,0:T(8,128)(2,1)} %get-tuple-element.95), calls=%async_computation | async-start | bytes 2097152 | tf_op jit(solution)/shard_map/all_to_all | solution.py:29
  138.9 137.6 %all-gather.7.cloned.1.call-start = ((), (), s32[]{:S(2)}) async-start(), calls=%async_computation.3 | async-start | bytes 3145728 | tf_op jit(solution)/shard_map/all_gather | solution.py:46
  149.7 6.4 %copy-start.6 = (bf16[384,288]{0,1:T(8,128)(2,1)S(1)}, bf16[384,288]{0,1:T(8,128)(2,1)}, u32[]{:S(2)}) copy-start(bf16[384,288]{0,1:T(8,128)(2,1)} %param.33) | copy-start | bytes 663556
  194.4 8.0 %copy-start.103 = (f32[8,3]{0,1:T(4,128)S(1)}, f32[8,3]{0,1:T(4,128)}, u32[]{:S(2)}) copy-start(f32[8,3]{0,1:T(4,128)} %copy.385) | copy-start | bytes 292
  194.4 8.1 %copy-start.86 = (f32[8]{0:T(128)S(1)}, f32[8]{0:T(128)}, u32[]{:S(2)}) copy-start(f32[8]{0:T(128)} %copy-done.85) | copy-start | bytes 100
  194.4 8.1 %copy-start.88 = (f32[8]{0:T(128)S(1)}, f32[8]{0:T(128)}, u32[]{:S(2)}) copy-start(f32[8]{0:T(128)} %copy-done.87) | copy-start | bytes 100
  194.4 8.1 %copy-start.90 = (f32[8]{0:T(128)S(1)}, f32[8]{0:T(128)}, u32[]{:S(2)}) copy-start(f32[8]{0:T(128)} %copy-done.89) | copy-start | bytes 100
  194.4 8.1 %copy-start.92 = (f32[8]{0:T(128)S(1)}, f32[8]{0:T(128)}, u32[]{:S(2)}) copy-start(f32[8]{0:T(128)} %copy-done.91) | copy-start | bytes 100
  194.4 8.1 %copy-start.94 = (f32[8]{0:T(128)S(1)}, f32[8]{0:T(128)}, u32[]{:S(2)}) copy-start(f32[8]{0:T(128)} %copy-done.93) | copy-start | bytes 100
  194.4 8.1 %copy-start.96 = (f32[8]{0:T(128)S(1)}, f32[8]{0:T(128)}, u32[]{:S(2)}) copy-start(f32[8]{0:T(128)} %copy-done.95) | copy-start | bytes 100
  194.4 8.1 %copy-start.98 = (f32[8]{0:T(128)S(1)}, f32[8]{0:T(128)}, u32[]{:S(2)}) copy-start(f32[8]{0:T(128)} %copy-done.97) | copy-start | bytes 100
  194.4 8.1 %copy-start.100 = (f32[8]{0:T(128)S(1)}, f32[8]{0:T(128)}, u32[]{:S(2)}) copy-start(f32[8]{0:T(128)} %copy-done.99) | copy-start | bytes 100
  194.4 8.1 %copy-start.102 = (f32[8]{0:T(128)S(1)}, f32[8]{0:T(128)}, u32[]{:S(2)}) copy-start(f32[8]{0:T(128)} %copy-done.101) | copy-start | bytes 100
  207.6 43.9 %copy-start.16 = (bf16[384,144]{0,1:T(8,128)(2,1)S(1)}, bf16[384,144]{0,1:T(8,128)(2,1)}, u32[]{:S(2)}) copy-start(bf16[384,144]{0,1:T(8,128)(2,1)} %param.31) | copy-start | bytes 331780
  207.6 44.8 %copy-start.14 = (bf16[384,192]{0,1:T(8,128)(2,1)S(1)}, bf16[384,192]{0,1:T(8,128)(2,1)}, u32[]{:S(2)}) copy-start(bf16[384,192]{0,1:T(8,128)(2,1)} %param.28) | copy-start | bytes 442372
  209.4 69.0 %copy-start.111 = (f32[8]{0:T(128)}, f32[8]{0:T(128)S(1)}, u32[]{:S(2)}) copy-start(f32[8]{0:T(128)S(1)} %get-tuple-element.69) | copy-start | bytes 100
  209.4 69.0 %copy-start.113 = (f32[8]{0:T(128)}, f32[8]{0:T(128)S(1)}, u32[]{:S(2)}) copy-start(f32[8]{0:T(128)S(1)} %get-tuple-element.169) | copy-start | bytes 100
  209.4 69.0 %copy-start.115 = (f32[8]{0:T(128)}, f32[8]{0:T(128)S(1)}, u32[]{:S(2)}) copy-start(f32[8]{0:T(128)S(1)} %get-tuple-element.173) | copy-start | bytes 100
  251.8 26.6 %copy-start.119 = (f32[8]{0:T(128)}, f32[8]{0:T(128)S(1)}, u32[]{:S(2)}) copy-start(f32[8]{0:T(128)S(1)} %get-tuple-element.194) | copy-start | bytes 100
  251.8 26.6 %copy-start.121 = (f32[8]{0:T(128)}, f32[8]{0:T(128)S(1)}, u32[]{:S(2)}) copy-start(f32[8]{0:T(128)S(1)} %get-tuple-element.195) | copy-start | bytes 100
  251.8 26.6 %copy-start.123 = (f32[8]{0:T(128)}, f32[8]{0:T(128)S(1)}, u32[]{:S(2)}) copy-start(f32[8]{0:T(128)S(1)} %get-tuple-element.196) | copy-start | bytes 100
  251.8 26.6 %copy-start.125 = (f32[8]{0:T(128)}, f32[8]{0:T(128)S(1)}, u32[]{:S(2)}) copy-start(f32[8]{0:T(128)S(1)} %get-tuple-element.197) | copy-start | bytes 100
  252.3 26.1 %copy-start.22 = (f32[8,1,48]{0,2,1:T(8,128)}, f32[8,1,48]{0,2,1:T(8,128)S(1)}, u32[]{:S(2)}) copy-start(f32[8,1,48]{0,2,1:T(8,128)S(1)} %copy.415) | copy-start | bytes 4612
  252.4 26.1 %copy-start.24 = (f32[8,1,48]{0,2,1:T(8,128)}, f32[8,1,48]{0,2,1:T(8,128)S(1)}, u32[]{:S(2)}) copy-start(f32[8,1,48]{0,2,1:T(8,128)S(1)} %copy.414) | copy-start | bytes 4612
  252.4 26.0 %copy-start.26 = (f32[8,1,48]{0,2,1:T(8,128)}, f32[8,1,48]{0,2,1:T(8,128)S(1)}, u32[]{:S(2)}) copy-start(f32[8,1,48]{0,2,1:T(8,128)S(1)} %copy.413) | copy-start | bytes 4612
  (103 other events, 231.3 us)
Sparse Core Ops, SparseCore 0:
  113.9 27.6 all-gather.4
  251.0 25.4 all-gather.6
where the time goes:
time: 308 us; the launch traced here: 307 us
  blocking collectives  111 us (36%)
  starting transfers between devices  55 us (18%)
  waiting for transfers between devices  50.5 us (16%)
  local copies, waits for them, and re-layouts  34.2 us (11%)
  matrix products  27.1 us (9%)
  between operations  16.2 us (5%)
  other arithmetic  13.2 us (4%)
    all_gather x4, blocking collectives, all_blocks(): pieces = lax.all_gather(pieces, axes[k], axis=0, tiled=True)  111 us
    all_to_all x2, starting transfers between devices, grouped_exchange(): lax.all_to_all(group, axis, split_axis=split_dim, concat_axis=concat_dim,...  54.7 us
    all_to_all x2, waiting for transfers between devices, grouped_exchange(): lax.all_to_all(group, axis, split_axis=split_dim, concat_axis=concat_dim,...  27.9 us
    all_gather x2, waiting for transfers between devices, all_blocks(): pieces = lax.all_gather(pieces, axes[k], axis=0, tiled=True)  22.5 us
  transfers between devices with their start and end apart: 4, of which 2 were waited for; matrix products, arithmetic and copies ran while one was open for 9% of the time, Pallas kernels for 0%

commit v1 on v0

v1 whole, which is shorter than its diff:
```python
import functools

import jax
import jax.numpy as jnp
from jax import lax
from jax.experimental import pallas as pl
from jax.experimental.pallas import tpu as pltpu
from jax.sharding import Mesh
from jax.sharding import PartitionSpec as P

LAYERS = 2
SPAN = 2
GROUPS_ROW = ("groups", "row_0", "row_1", "row_2")
LOGIT_WEIGHT = (1.0 / 3.0) ** 0.5
F32 = jnp.float32
BF16 = jnp.bfloat16
LANE = 128
HP = 16


def iota(shape, dim):
    return lax.broadcasted_iota(jnp.int32, shape, dim)


def dot(a, b):
    return jnp.dot(a, b, preferred_element_type=F32)


def dot_nt(a, b):
    return lax.dot_general(a, b, (((1,), (1,)), ((), ())), preferred_element_type=F32)


def split2(x):
    hi = x.astype(BF16)
    return hi, (x - hi.astype(F32)).astype(BF16)


def split3(x):
    hi = x.astype(BF16)
    rest = x - hi.astype(F32)
    mid = rest.astype(BF16)
    return hi, mid, (rest - mid.astype(F32)).astype(BF16)


def spread(x, table):
    hi, mid, lo = split3(x)
    return dot(hi, table) + dot(mid, table) + dot(lo, table)


def col(tile, lane):
    return jnp.broadcast_to(tile[:, lane : lane + 1], tile.shape)


def layer_norm(values, gain_vector):
    centered = values - jnp.mean(values, axis=-1, keepdims=True)
    variance = jnp.mean(centered * centered, axis=-1, keepdims=True)
    return centered * lax.rsqrt(variance + 1e-05) * gain_vector


def kernel(
    sizes,
    pair,
    single,
    rotation,
    translation,
    mask,
    chain,
    wq_hbm,
    wk_hbm,
    wv_hbm,
    wqp_hbm,
    wkp_hbm,
    wvp_hbm,
    pw_ref,
    hw_ref,
    cw_ref,
    wo_hbm,
    g1_ref,
    m1_hbm,
    m2_hbm,
    m3_hbm,
    g2_ref,
    fw_ref,
    out_state,
    out_frames,
    tile,
    kx,
    qx,
    xs,
    wqr,
    wkr,
    wvr,
    wqpr,
    wkpr,
    wvpr,
    wq,
    wk,
    wv,
    wo,
    m1,
    m2,
    m3,
    dec,
    expm,
    qf,
    kf,
    vh,
    vl,
    scores,
    bias,
    same,
    mh,
    me_mask,
    po,
    spb,
    ssb,
    pr,
    sr,
    w_sem,
    wo_sem,
    a2a_recv,
    a2a_send,
    x_send,
    kx_recv,
    qx_recv,
    p_send,
    s_send,
    p_recv,
    s_recv,
):
    nx, nb, cores, rows, heads = sizes
    g_count = nx * SPAN * cores
    nk = g_count * rows
    nq = nb * rows
    chan = single.shape[1]
    pq3 = wqp_hbm.shape[1]
    pqh = pq3 // 3
    pq = pqh // heads
    pv3 = wvp_hbm.shape[1]
    pvh = pv3 // 3
    pv = pvh // heads
    hd = wq_hbm.shape[1]
    dh = hd // heads
    vtail = LANE - pvh
    x = lax.axis_index("row_0")
    z = lax.axis_index("row_1")
    c = lax.axis_index("row_2")
    zb = z // SPAN
    zp = z % SPAN
    me = (x * SPAN + zp) * cores + c

    near = []
    for dx in (2, 1, 3, 0) if nx == 4 else range(nx):
        for dz in range(SPAN):
            for dc in range(cores):
                if dx or dz or dc:
                    near.append((dx, dz, dc))

    def near_id(offset):
        dx, dz, dc = offset
        return (x + dx) % nx, (zp + dz) % SPAN, (c + dc) % cores

    def dev(px, pz, pc):
        return {"row_0": px, "row_1": pz, "row_2": pc}

    def near_dev(offset):
        px, pzp, pc = near_id(offset)
        return dev(px, zb * SPAN + pzp, pc)

    def far_dev(block):
        return dev(x, block * SPAN + zp, c)

    def far_step(t):
        half = (t + 1) // 2
        sign = 1 - 2 * (t % 2)
        return (zb + nb // 2 + sign * half + nb) % nb

    barrier = pltpu.get_barrier_semaphore()
    for t in range(nb - 1):
        pl.semaphore_signal(
            barrier, inc=1, device_id=far_dev(far_step(t)), device_id_type=pl.DeviceIdType.MESH
        )
    for offset in near:
        pl.semaphore_signal(
            barrier, inc=1, device_id=near_dev(offset), device_id_type=pl.DeviceIdType.MESH
        )

    raw = [
        (wq_hbm, wqr),
        (wk_hbm, wkr),
        (wv_hbm, wvr),
        (wqp_hbm, wqpr),
        (wkp_hbm, wkpr),
        (wvp_hbm, wvpr),
        (m1_hbm, m1),
        (m2_hbm, m2),
        (m3_hbm, m3),
    ]
    raw_copies = [
        pltpu.make_async_copy(src, dst, w_sem.at[k]) for k, (src, dst) in enumerate(raw)
    ]
    for copy in raw_copies:
        copy.start()
    base_pt = hd
    base_norm = hd + pv3
    base_pair = base_norm + pvh
    wo_moves = [
        (base_pt, 0, pvh),
        (base_pt + pvh, LANE, pvh),
        (0, LANE + pvh, vtail),
        (base_pt + 2 * pvh, 2 * LANE, pvh),
        (vtail, 2 * LANE + pvh, vtail),
        (2 * vtail, 3 * LANE, hd - 2 * vtail),
        (base_norm, 4 * LANE, pvh),
        (base_pair, 5 * LANE, heads * LANE),
    ]
    wo[pvh:LANE, :] = jnp.zeros((vtail, chan), BF16)
    wo[4 * LANE + pvh : 5 * LANE, :] = jnp.zeros((vtail, chan), BF16)
    wo_copies = [
        pltpu.make_async_copy(
            wo_hbm.at[pl.ds(src, count)], wo.at[pl.ds(dst, count)], wo_sem.at[k]
        )
        for k, (src, dst, count) in enumerate(wo_moves)
    ]
    for copy in wo_copies:
        copy.start()

    lane8 = iota((rows, LANE), 1)
    take_r = (
        (iota((9, LANE), 1) % 12 == iota((9, LANE), 0)) & (iota((9, LANE), 1) < 36)
    ).astype(F32)
    take_t = (
        (iota((3, LANE), 1) % 12 == iota((3, LANE), 0) + 9) & (iota((3, LANE), 1) < 36)
    ).astype(F32)
    contract0 = (((0,), (0,)), ((), ()))
    frames = lax.dot_general(
        rotation[...], take_r, contract0, precision=lax.Precision.HIGHEST,
        preferred_element_type=F32,
    ) + lax.dot_general(
        translation[...], take_t, contract0, precision=lax.Precision.HIGHEST,
        preferred_element_type=F32,
    )

    def frame_columns(fr):
        hi = fr.astype(BF16).astype(F32)
        mid = (fr - hi).astype(BF16).astype(F32)
        lo = fr - hi - mid
        return jnp.where(lane8 < 12, hi, jnp.where(lane8 < 24, mid, lo)).astype(BF16)

    def put_message(layer, state_bf, fr):
        tail = frame_columns(fr)
        for ref in (xs.at[layer], kx.at[layer, me], qx.at[layer, zb]):
            ref[:, 0:chan] = state_bf
            ref[:, chan : chan + LANE] = tail

    def x_near(layer, offset):
        return pltpu.make_async_remote_copy(
            src_ref=xs.at[layer],
            dst_ref=kx.at[layer, me],
            send_sem=x_send.at[layer],
            recv_sem=kx_recv.at[layer],
            device_id=near_dev(offset),
            device_id_type=pl.DeviceIdType.MESH,
        )

    def x_far(layer, t):
        return pltpu.make_async_remote_copy(
            src_ref=xs.at[layer],
            dst_ref=qx.at[layer, zb],
            send_sem=x_send.at[layer],
            recv_sem=qx_recv.at[layer],
            device_id=far_dev(far_step(t)),
            device_id_type=pl.DeviceIdType.MESH,
        )

    def send_message(layer):
        for t in range(nb - 1):
            x_far(layer, t).start()
        for offset in near:
            x_near(layer, offset).start()

    put_message(0, single[...], frames)
    pl.semaphore_wait(barrier, len(near) + nb - 1)
    send_message(0)

    def a2a_step(t, carry):
        n = far_step(t)
        for offset in near:
            px, pzp, pc = near_id(offset)
            pltpu.make_async_remote_copy(
                src_ref=pair.at[px, n, pzp, pc],
                dst_ref=tile.at[n, :, pl.ds(me * rows, rows), :],
                send_sem=a2a_send,
                recv_sem=a2a_recv.at[n],
                device_id=dev(px, zb * SPAN + pzp, pc),
                device_id_type=pl.DeviceIdType.MESH,
            ).start()
        pltpu.make_async_copy(
            pair.at[x, n, zp, c], tile.at[n, :, pl.ds(me * rows, rows), :], a2a_recv.at[n]
        ).start()
        return carry

    lax.fori_loop(0, nb, a2a_step, 0)

    lane_row = iota((1, LANE), 1)

    def as_col(row):
        wide = jnp.broadcast_to(row, (HP, heads))
        pick = iota((HP, heads), 0) == iota((HP, heads), 1)
        return jnp.sum(jnp.where(pick, wide, 0.0), axis=1, keepdims=True)

    hw = hw_ref[...]
    soft = jnp.maximum(hw, 0.0) + jnp.log(1.0 + jnp.exp(-jnp.abs(hw)))
    w_col = as_col(soft * (2.0 / (9.0 * pq)) ** 0.5)
    cw_col = as_col(cw_ref[...])

    head_of = iota((HP, LANE), 0)
    lane_hp = iota((HP, LANE), 1)
    q_tail = hd - LANE
    qq0 = q_tail
    kk0 = q_tail + 2 * heads
    kk1 = kk0 + 3 * heads
    point_mask = ((lane_hp % pqh) // pq == head_of) & (lane_hp < 2 * pqh)
    tail_mask = ((lane_hp < q_tail) & ((lane_hp + LANE) // dh == head_of)) | (
        (lane_hp >= q_tail) & ((lane_hp - q_tail) % heads == head_of) & (lane_hp < kk1)
    )
    mh[:, 0:LANE] = (lane_hp // dh == head_of).astype(F32)
    mh[:, LANE : 2 * LANE] = tail_mask.astype(F32)
    for k in range(6):
        mh[:, (2 + k) * LANE : (3 + k) * LANE] = point_mask.astype(F32)
    v_mask = (lane_hp // pv == head_of) & (lane_hp < pvh)
    o_masks = [
        (lane_hp - pvh == head_of),
        ((lane_hp - pvh) // dh == head_of),
        ((lane_hp - pvh + vtail) // dh == head_of),
    ]
    for k in range(3):
        me_mask[:, k * LANE : (k + 1) * LANE] = (
            v_mask | ((lane_hp >= pvh) & o_masks[k])
        ).astype(F32)
    me_mask[:, 3 * LANE : 4 * LANE] = ((lane_hp + 2 * vtail) // dh == head_of).astype(F32)
    big_row = iota((LANE, 4 * LANE), 0) - pvh
    big_col = iota((LANE, 4 * LANE), 1)
    big_lane = big_col % LANE
    big_tile = big_col // LANE
    o_col = jnp.where(
        big_tile == 3, big_lane + 2 * vtail, big_lane - pvh + (big_tile - 1) * vtail
    )
    is_point = (big_tile < 3) & (big_lane < pvh)
    big_head = jnp.where(is_point, big_lane // pv, o_col // dh)
    has_head = is_point | (big_tile > 0)
    expm[...] = (
        (big_head == big_row) & has_head & (big_row >= 0) & (big_row < heads)
    ).astype(BF16)
    w_lane = jnp.sum(jnp.where(point_mask, w_col, 0.0), axis=0, keepdims=True)
    half_lane = -0.5 * jnp.sum(
        jnp.where((lane_hp - q_tail) % heads == head_of, w_col, 0.0), axis=0, keepdims=True
    )
    dec_row = iota((LANE, LANE), 0)
    for k in range(12):
        dec[:, k * LANE : (k + 1) * LANE] = ((dec_row % 12 == k) & (dec_row < 36)).astype(BF16)
    sel = (
        (iota((LANE, LANE), 0) < pqh)
        & (iota((LANE, LANE), 1) >= q_tail)
        & (iota((LANE, LANE), 1) < kk1)
        & ((iota((LANE, LANE), 1) - q_tail) % heads == iota((LANE, LANE), 0) // pq)
    ).astype(BF16)

    chain_v = chain[...]
    mask_v = mask[...]

    def total(values):
        return jnp.sum(
            jnp.sum(values.astype(F32), axis=1, keepdims=True), axis=0, keepdims=True
        )

    block_rows = SPAN * cores * rows
    key_local = iota((1, nk), 1)
    key_index = (
        (key_local // block_rows) * (nb * block_rows) + zb * block_rows + key_local % block_rows
    ).astype(F32)
    q_local = iota((nq, 1), 0)
    q_index = (
        x * (nb * block_rows)
        + (q_local // rows) * block_rows
        + (zp * cores + c) * rows
        + q_local % rows
    ).astype(F32)
    key_chain = jnp.zeros((1, nk), F32)
    q_chain = jnp.zeros((nq, 1), F32)
    for k in range(1, 4):
        edge = total(chain_v < k)
        key_chain = key_chain + (key_index >= edge).astype(F32)
        q_chain = q_chain + (q_index >= edge).astype(F32)
    same[...] = (q_chain == key_chain).astype(F32)
    pad_row = ((key_index < total(mask_v)).astype(F32) - 1.0) * 100000.0

    for copy in raw_copies:
        copy.wait()

    def perm(count, tile_index, width, copies):
        a = iota((count, LANE), 0)
        b = iota((count, LANE), 1)
        return ((a == tile_index * width + b % width) & (b < copies * width)).astype(BF16)

    for raw_w, raw_p, full, scale in ((wqr, wqpr, wq, 0.25), (wkr, wkpr, wk, 1.0)):
        full[:, 0:LANE] = raw_w[:, 0:LANE] * jnp.asarray(scale, BF16)
        full[:, LANE : 2 * LANE] = jnp.zeros((chan, LANE), BF16)
        full[:, LANE:hd] = raw_w[:, LANE:hd] * jnp.asarray(scale, BF16)
        for k in range(3):
            full[:, (2 + k) * LANE : (3 + k) * LANE] = dot(
                raw_p[...], perm(pq3, k, pqh, 2)
            ).astype(BF16)

    def v_pick(k):
        a = iota((hd, LANE), 0)
        b = iota((hd, LANE), 1)
        start = 2 * vtail if k == 3 else (k - 1) * vtail - pvh
        return ((a == b + start) & ((b >= pvh) | (k == 3))).astype(BF16)

    for k in range(4):
        acc = jnp.zeros((chan, LANE), F32)
        if k < 3:
            acc = acc + dot(wvpr[...], perm(pv3, k, pvh, 1))
        if k > 0:
            acc = acc + dot(wvr[...], v_pick(k))
        wv[:, k * LANE : (k + 1) * LANE] = acc.astype(BF16)

    pw16 = jnp.concatenate([pw_ref[...].astype(F32), jnp.zeros((HP - heads, LANE), F32)], axis=0)
    pw16 = pw16.astype(BF16)

    def global_points(px, py, pz, fb):
        def part(k):
            return fb[:, k * LANE : (k + 1) * LANE]

        return [
            part(3 * k) * px + part(3 * k + 1) * py + part(3 * k + 2) * pz + part(9 + k)
            for k in range(3)
        ]

    def tiles(values, start, count):
        return [values[:, (start + k) * LANE : (start + k + 1) * LANE] for k in range(count)]

    def key_phase(layer):
        message = kx[layer].reshape(nk, chan + LANE)
        fb = dot(message[:, chan:], dec[...])
        body = message[:, :chan]
        projected = dot(body, wk[...])
        lane = iota((nk, LANE), 1)
        g = global_points(*tiles(projected, 2, 3), fb)
        square = g[0] * g[0] + g[1] * g[1] + g[2] * g[2]
        kk = spread(square, sel) * half_lane
        hi = kk.astype(BF16).astype(F32)
        mid = (kk - hi).astype(BF16).astype(F32)
        lo = kk - hi - mid
        kk = jnp.where(lane < kk0 + heads, hi, jnp.where(lane < kk0 + 2 * heads, mid, lo))
        kk = jnp.where(lane < kk1, kk, 0.0)
        tail = jnp.where(
            lane < q_tail, projected[:, LANE : 2 * LANE], jnp.where(lane < kk0, 1.0, kk)
        )
        kf[:, 0:LANE] = projected[:, 0:LANE].astype(BF16)
        kf[:, LANE : 2 * LANE] = tail.astype(BF16)
        for k in range(3):
            hi = g[k].astype(BF16).astype(F32)
            pts = jnp.where(lane < pqh, hi, jnp.where(lane < 2 * pqh, g[k] - hi, 0.0)).astype(BF16)
            kf[:, (2 + k) * LANE : (3 + k) * LANE] = pts
            kf[:, (5 + k) * LANE : (6 + k) * LANE] = pts
        values = dot(body, wv[...])
        parts = tiles(values, 0, 4)
        g = global_points(parts[0], parts[1], parts[2], fb)
        for k in range(3):
            whole = jnp.where(lane < pvh, g[k], parts[k])
            hi = whole.astype(BF16)
            vh[:, k * LANE : (k + 1) * LANE] = hi
            vl[:, k * LANE : (k + 1) * LANE] = jnp.where(
                lane < pvh, whole - hi.astype(F32), 0.0
            ).astype(BF16)
        vh[:, 3 * LANE : 4 * LANE] = parts[3].astype(BF16)

    def query_phase(layer):
        message = qx[layer].reshape(nq, chan + LANE)
        fb = dot(message[:, chan:], dec[...])
        projected = dot(message[:, :chan], wq[...])
        lane = iota((nq, LANE), 1)
        g = global_points(*tiles(projected, 2, 3), fb)
        square = g[0] * g[0] + g[1] * g[1] + g[2] * g[2]
        qq = spread(square, sel) * half_lane
        hi = qq.astype(BF16).astype(F32)
        qq = jnp.where(lane < qq0 + heads, hi, qq - hi)
        tail = jnp.where(
            lane < q_tail,
            projected[:, LANE : 2 * LANE],
            jnp.where(lane < kk0, qq, jnp.where(lane < kk1, 1.0, 0.0)),
        )
        qf[:, 0:LANE] = projected[:, 0:LANE].astype(BF16).astype(F32)
        qf[:, LANE : 2 * LANE] = tail.astype(BF16).astype(F32)
        for k in range(3):
            scaled = g[k] * w_lane
            hi = scaled.astype(BF16).astype(F32)
            qf[:, (2 + k) * LANE : (3 + k) * LANE] = hi
            qf[:, (5 + k) * LANE : (6 + k) * LANE] = jnp.where(lane < pqh, scaled - hi, 0.0)

    group = 2 * rows

    def score_phase(layer):
        def step(j, carry):
            parts = []
            for r in range(group):
                row = qf[pl.ds(j * group + r, 1), :]
                parts.append((jnp.broadcast_to(row, (HP, 8 * LANE)) * mh[...]).astype(BF16))
            s = dot_nt(jnp.concatenate(parts, axis=0), kf[...])
            for r in range(group):
                match = jnp.broadcast_to(same[pl.ds(j * group + r, 1), :], (HP, nk))
                value = s[r * HP : (r + 1) * HP, :] * LOGIT_WEIGHT + match * cw_col + pad_row
                start = pl.multiple_of((j * group + r) * HP, HP)
                if layer > 0:
                    value = value + bias[pl.ds(start, HP), :]
                scores[pl.ds(start, HP), :] = value
            return carry

        lax.fori_loop(0, nq // group, step, 0)

    def p_copy(layer, n):
        return pltpu.make_async_remote_copy(
            src_ref=spb.at[layer, n],
            dst_ref=pr.at[layer, zb],
            send_sem=p_send.at[layer],
            recv_sem=p_recv.at[layer, zb],
            device_id=far_dev(n),
            device_id_type=pl.DeviceIdType.MESH,
        )

    def s_copy(layer, n):
        return pltpu.make_async_remote_copy(
            src_ref=ssb.at[layer, n],
            dst_ref=sr.at[layer, zb],
            send_sem=s_send.at[layer],
            recv_sem=s_recv.at[layer, zb],
            device_id=far_dev(n),
            device_id_type=pl.DeviceIdType.MESH,
        )

    def chunk_phase(layer):
        def chunk(t):
            n = far_step(t)
            if layer == 0:
                pltpu.make_async_copy(tile.at[n], tile.at[n], a2a_recv.at[n]).wait()
            weights = []
            inverses = []
            sums = []
            for r in range(rows):
                start = pl.multiple_of((n * rows + r) * HP, HP)
                logits = scores[pl.ds(start, HP), :]
                pair_rows = tile[n, r]
                if layer == 0:
                    own_bias = dot_nt(pw16, pair_rows) * LOGIT_WEIGHT
                    bias[pl.ds(start, HP), :] = own_bias
                    logits = logits + own_bias
                top = jnp.max(logits, axis=1, keepdims=True)
                p = jnp.exp(logits - top)
                count = jnp.sum(p, axis=1, keepdims=True)
                p = p.astype(BF16)
                inverse = 1.0 / count
                po[r * HP : (r + 1) * HP, :] = dot(p, pair_rows) * inverse
                weights.append(p)
                inverses.append(inverse)
                sums.append(top + jnp.log(count))
            p_all = jnp.concatenate(weights, axis=0)
            main = dot(p_all, vh[...])
            rest = dot(p_all, vl[...])
            for r in range(rows):
                low = r * HP
                for k in range(4):
                    value = main[low : low + HP, k * LANE : (k + 1) * LANE]
                    if k < 3:
                        value = value + rest[low : low + HP, k * LANE : (k + 1) * LANE]
                    value = value * inverses[r]
                    if k == 0:
                        value = jnp.where(lane_hp < pvh, value, sums[r])
                    value = value * me_mask[:, k * LANE : (k + 1) * LANE]
                    ssb[layer, n, r : r + 1, k * LANE : (k + 1) * LANE] = jnp.sum(
                        value, axis=0, keepdims=True
                    )
            for h in range(heads):
                spb[layer, n, h] = po[pl.ds(h, rows, stride=HP), :].astype(BF16)
            return n

        def step(t, carry):
            n = chunk(t)
            p_copy(layer, n).start()
            s_copy(layer, n).start()
            return carry

        lax.fori_loop(0, nb - 1, step, 0)
        chunk(nb - 1)

    valid = (lane8 >= pvh) & (lane8 < pvh + heads)

    def combine(layer):
        small = [ssb[layer, zb]]
        slots = [zb]
        for d in range(1, nb):
            n = (zb + d) % nb
            slots.append(n)
            pltpu.make_async_copy(
                sr.at[layer, n], sr.at[layer, n], s_recv.at[layer, n]
            ).wait()
            small.append(sr[layer, n])
        sums = [jnp.where(valid, value[:, 0:LANE], 0.0) for value in small]
        top = functools.reduce(jnp.maximum, sums)
        shares = [jnp.where(valid, jnp.exp(value - top), 0.0) for value in sums]
        whole = jnp.where(valid, functools.reduce(jnp.add, shares), 1.0)
        shares = [value / whole for value in shares]
        wide = spread(jnp.concatenate(shares, axis=0), expm[...])
        mixed = functools.reduce(
            jnp.add, [wide[d * rows : (d + 1) * rows, :] * small[d] for d in range(nb)]
        )
        for d in range(1, nb):
            pltpu.make_async_copy(
                pr.at[layer, slots[d]], pr.at[layer, slots[d]], p_recv.at[layer, slots[d]]
            ).wait()
        pairs = []
        for h in range(heads):
            acc = None
            for d in range(nb):
                part = spb[layer, zb, h] if d == 0 else pr[layer, slots[d], h]
                term = col(shares[d], pvh + h) * part.astype(F32)
                acc = term if acc is None else acc + term
            pairs.append(acc)
        return mixed, pairs

    def update(layer, state, fr, mixed, pairs):
        turn = [col(fr, k) for k in range(9)]
        shift = [col(fr, 9 + k) for k in range(3)]
        mix = tiles(mixed, 0, 4)
        moved = [mix[k] - shift[k] for k in range(3)]
        local = [
            turn[k] * moved[0] + turn[3 + k] * moved[1] + turn[6 + k] * moved[2] for k in range(3)
        ]
        inside = lane8 < pvh
        norm = jnp.sqrt(
            local[0] * local[0] + local[1] * local[1] + local[2] * local[2] + 1e-08
        )
        concat = [
            jnp.where(inside, local[0], 0.0),
            jnp.where(inside, local[1], mix[1]),
            jnp.where(inside, local[2], mix[2]),
            mix[3],
            jnp.where(inside, norm, 0.0),
        ] + pairs
        concat = jnp.concatenate(concat, axis=1).astype(BF16)
        if layer == 0:
            for copy in wo_copies:
                copy.wait()
        state = state + dot(concat, wo[...])
        normed = layer_norm(state, g1_ref[...])
        hidden = jnp.maximum(dot(normed.astype(BF16), m1[...]), 0.0).astype(BF16)
        hidden = jnp.maximum(dot(hidden, m2[...]), 0.0).astype(BF16)
        state = layer_norm(normed + dot(hidden, m3[...]), g2_ref[...])
        state_bf = state.astype(BF16)
        upd = dot(state_bf, fw_ref[...])
        u = [jnp.broadcast_to(upd[:, k : k + 1], (rows, LANE)) for k in range(6)]
        inverse = lax.rsqrt(1.0 + u[0] * u[0] + u[1] * u[1] + u[2] * u[2])
        vx, vy, vz = u[0] * inverse, u[1] * inverse, u[2] * inverse
        square = inverse * inverse
        matrix = [
            [
                square + vx * vx - vy * vy - vz * vz,
                2.0 * (vx * vy - inverse * vz),
                2.0 * (vx * vz + inverse * vy),
            ],
            [
                2.0 * (vx * vy + inverse * vz),
                square - vx * vx + vy * vy - vz * vz,
                2.0 * (vy * vz - inverse * vx),
            ],
            [
                2.0 * (vx * vz - inverse * vy),
                2.0 * (vy * vz + inverse * vx),
                square - vx * vx - vy * vy + vz * vz,
            ],
        ]
        entries = [
            turn[3 * a] * matrix[0][b]
            + turn[3 * a + 1] * matrix[1][b]
            + turn[3 * a + 2] * matrix[2][b]
            for a in range(3)
            for b in range(3)
        ] + [
            turn[3 * a] * u[3] + turn[3 * a + 1] * u[4] + turn[3 * a + 2] * u[5] + shift[a]
            for a in range(3)
        ]
        fr = jnp.zeros((rows, LANE), F32)
        for k in range(12):
            fr = jnp.where((lane8 % 12 == k) & (lane8 < 36), entries[k], fr)
        return state, state_bf, fr

    state = single[...].astype(F32)
    for layer in range(LAYERS):
        pltpu.make_async_copy(
            kx.at[layer, 0 : g_count - 1], kx.at[layer, 0 : g_count - 1], kx_recv.at[layer]
        ).wait()
        key_phase(layer)
        pltpu.make_async_copy(
            qx.at[layer, 0 : nb - 1], qx.at[layer, 0 : nb - 1], qx_recv.at[layer]
        ).wait()
        query_phase(layer)
        score_phase(layer)
        chunk_phase(layer)
        mixed, pairs = combine(layer)
        state, state_bf, frames = update(layer, state, frames, mixed, pairs)
        if layer + 1 < LAYERS:
            put_message(layer + 1, state_bf, frames)
            send_message(layer + 1)
    out_state[...] = state
    out_frames[...] = frames

    for layer in range(LAYERS):
        pltpu.make_async_copy(
            kx.at[layer, 0 : g_count - 1], kx.at[layer, 0 : g_count - 1], x_send.at[layer]
        ).wait()
        pltpu.make_async_copy(
            qx.at[layer, 0 : nb - 1], qx.at[layer, 0 : nb - 1], x_send.at[layer]
        ).wait()
        pltpu.make_async_copy(
            pr.at[layer, 0 : nb - 1], pr.at[layer, 0 : nb - 1], p_send.at[layer]
        ).wait()
        pltpu.make_async_copy(
            sr.at[layer, 0 : nb - 1], sr.at[layer, 0 : nb - 1], s_send.at[layer]
        ).wait()
    for offset in near:
        px, pzp, pc = near_id(offset)
        pltpu.make_async_copy(pair.at[px, :, pzp, pc], pair.at[px, :, pzp, pc], a2a_send).wait()


def on_device(
    pair_cols,
    single,
    rotation,
    translation,
    residue_mask,
    chain_index,
    query_weight,
    key_weight,
    value_weight,
    qpoint_weight,
    kpoint_weight,
    vpoint_weight,
    pair_weight,
    head_weight,
    chain_weight,
    output_weight,
    gain_first,
    mlp_first,
    mlp_second,
    mlp_third,
    gain_second,
    frame_weight,
):
    nx = lax.axis_size("row_0")
    nz = lax.axis_size("row_1")
    cores = lax.axis_size("row_2")
    nb = nz // SPAN
    rows, chan = single.shape
    heads = head_weight.shape[0]
    hd = query_weight.shape[1]
    g_count = nx * SPAN * cores
    nk = g_count * rows
    nq = nb * rows
    width = chan + LANE
    pair = pair_cols.reshape(nx, nb, SPAN, cores, rows, *pair_cols.shape[1:])
    vmem = pl.BlockSpec(memory_space=pltpu.VMEM)
    hbm = pl.BlockSpec(memory_space=pl.ANY)
    in_specs = [hbm] + [vmem] * 5 + [hbm] * 6 + [vmem] * 3 + [hbm, vmem] + [hbm] * 3 + [vmem] * 2
    scratch = [
        pltpu.VMEM((nb, rows, nk, LANE), BF16),
        pltpu.VMEM((LAYERS, g_count, rows, width), BF16),
        pltpu.VMEM((LAYERS, nb, rows, width), BF16),
        pltpu.VMEM((LAYERS, rows, width), BF16),
        pltpu.VMEM(query_weight.shape, BF16),
        pltpu.VMEM(key_weight.shape, BF16),
        pltpu.VMEM(value_weight.shape, BF16),
        pltpu.VMEM(qpoint_weight.shape, BF16),
        pltpu.VMEM(kpoint_weight.shape, BF16),
        pltpu.VMEM(vpoint_weight.shape, BF16),
        pltpu.VMEM((chan, 5 * LANE), BF16),
        pltpu.VMEM((chan, 5 * LANE), BF16),
        pltpu.VMEM((chan, 4 * LANE), BF16),
        pltpu.VMEM(((5 + heads) * LANE, chan), BF16),
        pltpu.VMEM(mlp_first.shape, BF16),
        pltpu.VMEM(mlp_second.shape, BF16),
        pltpu.VMEM(mlp_third.shape, BF16),
        pltpu.VMEM((LANE, 12 * LANE), BF16),
        pltpu.VMEM((LANE, 4 * LANE), BF16),
        pltpu.VMEM((nq, 8 * LANE), F32),
        pltpu.VMEM((nk, 8 * LANE), BF16),
        pltpu.VMEM((nk, 4 * LANE), BF16),
        pltpu.VMEM((nk, 3 * LANE), BF16),
        pltpu.VMEM((nq * HP, nk), F32),
        pltpu.VMEM((nq * HP, nk), F32),
        pltpu.VMEM((nq, nk), F32),
        pltpu.VMEM((HP, 8 * LANE), F32),
        pltpu.VMEM((HP, 4 * LANE), F32),
        pltpu.VMEM((rows * HP, LANE), F32),
        pltpu.VMEM((LAYERS, nb, heads, rows, LANE), BF16),
        pltpu.VMEM((LAYERS, nb, rows, 4 * LANE), F32),
        pltpu.VMEM((LAYERS, nb, heads, rows, LANE), BF16),
        pltpu.VMEM((LAYERS, nb, rows, 4 * LANE), F32),
        pltpu.SemaphoreType.DMA((9,)),
        pltpu.SemaphoreType.DMA((8,)),
        pltpu.SemaphoreType.DMA((nb,)),
        pltpu.SemaphoreType.DMA,
        pltpu.SemaphoreType.DMA((LAYERS,)),
        pltpu.SemaphoreType.DMA((LAYERS,)),
        pltpu.SemaphoreType.DMA((LAYERS,)),
        pltpu.SemaphoreType.DMA((LAYERS,)),
        pltpu.SemaphoreType.DMA((LAYERS,)),
        pltpu.SemaphoreType.DMA((LAYERS, nb)),
        pltpu.SemaphoreType.DMA((LAYERS, nb)),
    ]
    state, frames = pl.pallas_call(
        functools.partial(kernel, (nx, nb, cores, rows, heads)),
        name="structure_layers",
        out_shape=(
            jax.ShapeDtypeStruct((rows, chan), F32),
            jax.ShapeDtypeStruct((rows, LANE), F32),
        ),
        in_specs=in_specs,
        out_specs=(vmem, vmem),
        scratch_shapes=scratch,
        compiler_params=pltpu.CompilerParams(
            collective_id=0, has_side_effects=True, vmem_limit_bytes=48 * 1024 * 1024
        ),
    )(
        pair,
        single,
        rotation,
        translation,
        residue_mask.reshape(-1, LANE),
        chain_index.reshape(-1, LANE),
        query_weight,
        key_weight,
        value_weight,
        qpoint_weight,
        kpoint_weight,
        vpoint_weight,
        pair_weight,
        head_weight.reshape(1, -1),
        chain_weight.reshape(1, -1),
        output_weight,
        gain_first.reshape(1, -1),
        mlp_first,
        mlp_second,
        mlp_third,
        gain_second.reshape(1, -1),
        frame_weight,
    )
    return state, jnp.transpose(frames[:, :9]), jnp.transpose(frames[:, 9:12])


def solution(mesh):
    finer = Mesh(
        mesh.devices.reshape(mesh.shape["groups"], 4, 16, 2), ("groups", "row_0", "row_1", "row_2")
    )
    in_specs = (
        P(None, GROUPS_ROW, None),
        P(GROUPS_ROW, None),
        P(None, GROUPS_ROW),
        P(None, GROUPS_ROW),
        P("groups"),
        P("groups"),
    ) + (P(),) * 16
    out_specs = (P(GROUPS_ROW, None), P(None, GROUPS_ROW), P(None, GROUPS_ROW))
    return jax.shard_map(
        on_device, mesh=finer, in_specs=in_specs, out_specs=out_specs, check_vma=False
    )
```

time: 308 us -> 117 us (0.38)
  blocking collectives: 111 us -> 0 us
  Pallas kernels: 0 us -> 99.5 us
  starting transfers between devices: 55 us -> 0 us
  waiting for transfers between devices: 50.5 us -> 0 us
  matrix products: 27.1 us -> 0 us
  local copies, waits for them, and re-layouts: 34.2 us -> 15.8 us
  between operations: 16.2 us -> 0.81 us
  other arithmetic: 13.2 us -> 0 us
    all_gather x4 -> x0, blocking collectives: 111 us -> none  [all_blocks(): pieces = lax.all_gather(pieces, axes[k], axis=0, tiled=True)]
    pallas_call x0 -> x1, Pallas kernels: none -> 99.5 us  [on_device(): pl.pallas_call(functools.partial(kernel, (nx, nb, cores, rows, heads)), n...]
    all_to_all x2 -> x0, starting transfers between devices: 54.7 us -> none  [grouped_exchange(): lax.all_to_all(group, axis, split_axis=split_dim, concat_axis=concat_dim,...]
    all_to_all x2 -> x0, waiting for transfers between devices: 27.9 us -> none  [grouped_exchange(): lax.all_to_all(group, axis, split_axis=split_dim, concat_axis=concat_dim,...]
    dot_general x30 -> x0, matrix products: 23.1 us -> none  [the longest x2 4.57 us: attend(): jnp.einsum('ihj,jkhp->ikhp', attention.astype(jnp.float32), value_pts, pr...]
    all_gather x2 -> x0, waiting for transfers between devices: 22.5 us -> none  [all_blocks(): pieces = lax.all_gather(pieces, axes[k], axis=0, tiled=True)]
    slice x7 -> x0, local copies, waits for them, and re-layouts: 10.2 us -> none  [the longest x3 4.4 us: to_global(): translation[component][:, None]]
    unnamed x302 -> x34, local copies, waits for them, and re-layouts: 5.55 us -> 13.6 us
  transfers between devices with their start and end apart: 4 -> 0, of which waited for: 2 -> 0; matrix products, arithmetic and copies ran while one was open for 9% -> 0% of each run, Pallas kernels for 0% -> 0%
where the time goes in v1:
time: 117 us; the launch traced here: 116 us
  Pallas kernels  99.5 us (85%)
  local copies, waits for them, and re-layouts  15.8 us (14%)
    pallas_call x1, Pallas kernels, on_device(): pl.pallas_call(functools.partial(kernel, (nx, nb, cores, rows, heads)), n...  99.5 us
    unnamed x34, local copies, waits for them, and re-layouts  13.6 us

profile of v1, /device:TPU:33, one launch (start us, length us, event | category | flops | bytes accessed | tf_op | source)
XLA Modules:
  0.0 116.1 jit_solution(4343208251679282242)
XLA Ops:
  0.6 0.0 copy-start.11
  0.6 0.0 copy-start.10
  0.7 0.0 copy-start.8
  0.7 0.0 copy-start.7
  0.7 0.0 copy-start.6
  0.7 0.0 copy-start.9
  0.7 0.0 copy-start.5
  0.7 0.0 copy-start
  0.7 0.8 reshape.32.g1_ref
  1.5 0.7 reshape.33.g2_ref
  2.2 0.8 copy.25.rotation
  3.0 0.9 copy.32.fw_ref
  3.9 1.1 copy.26.wq_hbm
  4.9 1.0 copy.27.wk_hbm
  6.0 1.0 copy.28.wv_hbm
  7.0 1.0 copy.29.wqp_hbm
  8.1 1.0 copy.30.wkp_hbm
  9.1 1.1 copy.31.wvp_hbm
  10.2 0.0 copy-done.11
  10.3 0.0 copy-done.10
  10.3 0.0 copy-done.8
  10.3 0.0 copy-done.7
  10.3 0.0 copy-done.6
  10.3 0.0 copy-done.9
  10.3 0.0 copy-done.5
  10.3 0.0 copy-done
  10.3 0.0 copy-start.1
  10.3 1.4 %copy-done.1 = bf16[2112,384]{1,0:T(8,128)(2,1)S(1)} copy-done((bf16[2112,384]{1,0:T(8,128)(2,1)S(1)}, bf16[2112,384]{1,0:T(8,128)(2,1)}, u32[]{:S(2)}) %copy-start.1) | copy-done | bytes 1622040
  11.8 0.0 copy-start.2
  11.8 1.0 copy-done.2
  12.7 0.0 copy-start.3
  12.7 1.0 copy-done.3
  13.7 0.0 copy-start.4
  13.7 1.0 copy-done.4
  14.6 99.5 %structure_layers.1 = (f32[8,384]{1,0:T(8,128)S(1)}, f32[8,128]{1,0:T(8,128)S(1)}) custom-call(bf16[4,8,2,2,8,8,128]{6,5,4,3,2,1,0:T(8,128)(2,1)S(1)} %bitcast.9, bf16[8,384]{1,0:T(8,128)(2,1)S(1)} %copy-done.5, f32[9,8]{1,0:T(8,128)S(1)} %copy.25.rotation, f32[3,8]{1,0:T(4,128)S(1)} %copy-done.9, s32[8,128]{1,0:T(8,128)S(1)} %bitcast.10, ...), custom_call_target="tpu_custom_call" | custom-call | tf_op jit(solution)/shard_map/structure_layers/pallas_call | solution.py:821
  114.1 0.1 slice_bitcast_fusion
  114.2 0.7 copy.33
  114.9 0.6 slice_bitcast_fusion.1
  115.5 0.6 copy.35
Async XLA Ops:
  0.6 9.6 %copy-start.11 = (f32[12]{0:T(128)S(1)}, f32[12]{0:T(128)}, u32[]{:S(2)}) copy-start(f32[12]{0:T(128)} %param.36) | copy-start | bytes 148
  0.6 9.6 %copy-start.10 = (f32[12]{0:T(128)S(1)}, f32[12]{0:T(128)}, u32[]{:S(2)}) copy-start(f32[12]{0:T(128)} %param.35) | copy-start | bytes 148
  0.7 9.6 %copy-start.8 = (bf16[12,128]{1,0:T(8,128)(2,1)S(1)}, bf16[12,128]{1,0:T(8,128)(2,1)}, u32[]{:S(2)}) copy-start(bf16[12,128]{1,0:T(8,128)(2,1)} %pw_ref.1) | copy-start | bytes 9220
  0.7 9.6 %copy-start.7 = (s32[1024]{0:T(1024)S(1)}, s32[1024]{0:T(1024)}, u32[]{:S(2)}) copy-start(s32[1024]{0:T(1024)} %param.27) | copy-start | bytes 12292
  0.7 9.6 %copy-start.6 = (s32[1024]{0:T(1024)S(1)}, s32[1024]{0:T(1024)}, u32[]{:S(2)}) copy-start(s32[1024]{0:T(1024)} %param.26) | copy-start | bytes 12292
  0.7 9.6 %copy-start.9 = (f32[3,8]{1,0:T(4,128)S(1)}, f32[3,8]{1,0:T(4,128)}, u32[]{:S(2)}) copy-start(f32[3,8]{1,0:T(4,128)} %translation.1) | copy-start | bytes 292
  0.7 9.6 %copy-start.5 = (bf16[8,384]{1,0:T(8,128)(2,1)S(1)}, bf16[8,384]{1,0:T(8,128)(2,1)}, u32[]{:S(2)}) copy-start(bf16[8,384]{1,0:T(8,128)(2,1)} %single.1) | copy-start | bytes 18436
  0.7 9.6 %copy-start = (bf16[1024,8,128]{2,1,0:T(8,128)(2,1)S(1)}, bf16[1024,8,128]{2,1,0:T(8,128)(2,1)}, u32[]{:S(2)}) copy-start(bf16[1024,8,128]{2,1,0:T(8,128)(2,1)} %param.22) | copy-start | bytes 6291460
  10.3 1.4 %copy-start.1 = (bf16[2112,384]{1,0:T(8,128)(2,1)S(1)}, bf16[2112,384]{1,0:T(8,128)(2,1)}, u32[]{:S(2)}) copy-start(bf16[2112,384]{1,0:T(8,128)(2,1)} %wo_hbm.1) | copy-start | bytes 4866052
  11.8 1.0 copy-start.2
  12.7 1.0 copy-start.3
  13.7 1.0 copy-start.4

commit v2 on v1

--- a/solution.py
+++ b/solution.py
@@ -82,17 +82,15 @@
     g2_ref,
     fw_ref,
     out_state,
-    out_frames,
+    out_turn,
+    out_shift,
     tile,
     kx,
     qx,
     xs,
-    wqr,
-    wkr,
-    wvr,
-    wqpr,
-    wkpr,
-    wvpr,
+    wqt,
+    wkt,
+    wvt,
     wq,
     wk,
     wv,
@@ -112,10 +110,10 @@
     mh,
     me_mask,
     po,
+    sm,
+    fq,
     spb,
-    ssb,
     pr,
-    sr,
     w_sem,
     wo_sem,
     a2a_recv,
@@ -124,31 +122,36 @@
     kx_recv,
     qx_recv,
     p_send,
-    s_send,
     p_recv,
-    s_recv,
 ):
     nx, nb, cores, rows, heads = sizes
     g_count = nx * SPAN * cores
     nk = g_count * rows
     nq = nb * rows
     chan = single.shape[1]
-    pq3 = wqp_hbm.shape[1]
+    pq3 = wqp_hbm.shape[0]
     pqh = pq3 // 3
     pq = pqh // heads
-    pv3 = wvp_hbm.shape[1]
+    pv3 = wvp_hbm.shape[0]
     pvh = pv3 // 3
     pv = pvh // heads
-    hd = wq_hbm.shape[1]
+    hd = wq_hbm.shape[0]
     dh = hd // heads
     vtail = LANE - pvh
     x = lax.axis_index("row_0")
     z = lax.axis_index("row_1")
     c = lax.axis_index("row_2")
+    nz = nb * SPAN
     zb = z // SPAN
     zp = z % SPAN
-    me = (x * SPAN + zp) * cores + c
-
+
+    def partner(core):
+        return (z + 1 - 2 * ((z + core) % SPAN) + nz) % nz
+
+    def place(core):
+        return (x * SPAN + (z + core) % SPAN) * cores + c
+
+    me = place(c)
     near = []
     for dx in (2, 1, 3, 0) if nx == 4 else range(nx):
         for dz in range(SPAN):
@@ -158,14 +161,15 @@
 
     def near_id(offset):
         dx, dz, dc = offset
-        return (x + dx) % nx, (zp + dz) % SPAN, (c + dc) % cores
+        core = (c + dc) % cores
+        return (x + dx) % nx, partner(core) if dz else z, core
+
+    def source_id(offset):
+        dx, dz, dc = offset
+        return (x + dx) % nx, partner(c) if dz else z, (c + dc) % cores
 
     def dev(px, pz, pc):
         return {"row_0": px, "row_1": pz, "row_2": pc}
-
-    def near_dev(offset):
-        px, pzp, pc = near_id(offset)
-        return dev(px, zb * SPAN + pzp, pc)
 
     def far_dev(block):
         return dev(x, block * SPAN + zp, c)
@@ -182,22 +186,39 @@
         )
     for offset in near:
         pl.semaphore_signal(
-            barrier, inc=1, device_id=near_dev(offset), device_id_type=pl.DeviceIdType.MESH
-        )
-
-    raw = [
-        (wq_hbm, wqr),
-        (wk_hbm, wkr),
-        (wv_hbm, wvr),
-        (wqp_hbm, wqpr),
-        (wkp_hbm, wkpr),
-        (wvp_hbm, wvpr),
-        (m1_hbm, m1),
-        (m2_hbm, m2),
-        (m3_hbm, m3),
+            barrier,
+            inc=1,
+            device_id=dev(*source_id(offset)),
+            device_id_type=pl.DeviceIdType.MESH,
+        )
+
+    moves = [(wq_hbm, 0, wqt, 0, hd), (wk_hbm, 0, wkt, 0, hd)]
+    for src, dst in ((wqp_hbm, wqt), (wkp_hbm, wkt)):
+        for k in range(3):
+            for copy_index in range(2):
+                moves.append((src, k * pqh, dst, (2 + k) * LANE + copy_index * pqh, pqh))
+    for k in range(3):
+        moves.append((wvp_hbm, k * pvh, wvt, k * LANE, pvh))
+    moves += [
+        (wv_hbm, 0, wvt, LANE + pvh, vtail),
+        (wv_hbm, vtail, wvt, 2 * LANE + pvh, vtail),
+        (wv_hbm, 2 * vtail, wvt, 3 * LANE, hd - 2 * vtail),
+        (m1_hbm, 0, m1, 0, chan),
+        (m2_hbm, 0, m2, 0, chan),
+        (m3_hbm, 0, m3, 0, chan),
     ]
+    for ref in (wqt, wkt):
+        ref[hd : 2 * LANE, :] = jnp.zeros((2 * LANE - hd, chan), BF16)
+        for k in range(3):
+            ref[(2 + k) * LANE + 2 * pqh : (3 + k) * LANE, :] = jnp.zeros(
+                (LANE - 2 * pqh, chan), BF16
+            )
+    wvt[pvh:LANE, :] = jnp.zeros((vtail, chan), BF16)
     raw_copies = [
-        pltpu.make_async_copy(src, dst, w_sem.at[k]) for k, (src, dst) in enumerate(raw)
+        pltpu.make_async_copy(
+            src.at[pl.ds(start, count)], dst.at[pl.ds(into, count)], w_sem.at[k]
+        )
+        for k, (src, start, dst, into, count) in enumerate(moves)
     ]
     for copy in raw_copies:
         copy.start()
@@ -233,9 +254,8 @@
         (iota((3, LANE), 1) % 12 == iota((3, LANE), 0) + 9) & (iota((3, LANE), 1) < 36)
     ).astype(F32)
     contract0 = (((0,), (0,)), ((), ()))
-    frames = lax.dot_general(
-        rotation[...], take_r, contract0, precision=lax.Precision.HIGHEST,
-        preferred_element_type=F32,
+    frames = jnp.dot(
+        rotation[...], take_r, precision=lax.Precision.HIGHEST, preferred_element_type=F32
     ) + lax.dot_general(
         translation[...], take_t, contract0, precision=lax.Precision.HIGHEST,
         preferred_element_type=F32,
@@ -254,12 +274,13 @@
             ref[:, chan : chan + LANE] = tail
 
     def x_near(layer, offset):
+        target = near_id(offset)
         return pltpu.make_async_remote_copy(
             src_ref=xs.at[layer],
-            dst_ref=kx.at[layer, me],
+            dst_ref=kx.at[layer, place(target[2])],
             send_sem=x_send.at[layer],
             recv_sem=kx_recv.at[layer],
-            device_id=near_dev(offset),
+            device_id=dev(*target),
             device_id_type=pl.DeviceIdType.MESH,
         )
 
@@ -280,19 +301,20 @@
             x_near(layer, offset).start()
 
     put_message(0, single[...], frames)
-    pl.semaphore_wait(barrier, len(near) + nb - 1)
+    with jax.named_scope("barrier"):
+        pl.semaphore_wait(barrier, len(near) + nb - 1)
     send_message(0)
 
     def a2a_step(t, carry):
         n = far_step(t)
         for offset in near:
-            px, pzp, pc = near_id(offset)
+            px, pz, pc = near_id(offset)
             pltpu.make_async_remote_copy(
-                src_ref=pair.at[px, n, pzp, pc],
-                dst_ref=tile.at[n, :, pl.ds(me * rows, rows), :],
+                src_ref=pair.at[px, n, pz % SPAN, pc],
+                dst_ref=tile.at[n, :, pl.ds(place(pc) * rows, rows), :],
                 send_sem=a2a_send,
                 recv_sem=a2a_recv.at[n],
-                device_id=dev(px, zb * SPAN + pzp, pc),
+                device_id=dev(px, pz, pc),
                 device_id_type=pl.DeviceIdType.MESH,
             ).start()
         pltpu.make_async_copy(
@@ -300,7 +322,8 @@
         ).start()
         return carry
 
-    lax.fori_loop(0, nb, a2a_step, 0)
+    with jax.named_scope("exchange"):
+        lax.fori_loop(0, nb, a2a_step, 0)
 
     lane_row = iota((1, LANE), 1)
 
@@ -330,7 +353,7 @@
         mh[:, (2 + k) * LANE : (3 + k) * LANE] = point_mask.astype(F32)
     v_mask = (lane_hp // pv == head_of) & (lane_hp < pvh)
     o_masks = [
-        (lane_hp - pvh == head_of),
+        ((lane_hp - pvh) % heads == head_of) & (lane_hp < pvh + 2 * heads),
         ((lane_hp - pvh) // dh == head_of),
         ((lane_hp - pvh + vtail) // dh == head_of),
     ]
@@ -374,10 +397,12 @@
             jnp.sum(values.astype(F32), axis=1, keepdims=True), axis=0, keepdims=True
         )
 
-    block_rows = SPAN * cores * rows
+    plane_rows = cores * rows
+    block_rows = SPAN * plane_rows
     key_local = iota((1, nk), 1)
+    key_plane = (z - (z + c) % SPAN + (key_local // plane_rows) % SPAN + nz) % nz
     key_index = (
-        (key_local // block_rows) * (nb * block_rows) + zb * block_rows + key_local % block_rows
+        ((key_local // block_rows) * nz + key_plane) * plane_rows + key_local % plane_rows
     ).astype(F32)
     q_local = iota((nq, 1), 0)
     q_index = (
@@ -397,34 +422,9 @@
 
     for copy in raw_copies:
         copy.wait()
-
-    def perm(count, tile_index, width, copies):
-        a = iota((count, LANE), 0)
-        b = iota((count, LANE), 1)
-        return ((a == tile_index * width + b % width) & (b < copies * width)).astype(BF16)
-
-    for raw_w, raw_p, full, scale in ((wqr, wqpr, wq, 0.25), (wkr, wkpr, wk, 1.0)):
-        full[:, 0:LANE] = raw_w[:, 0:LANE] * jnp.asarray(scale, BF16)
-        full[:, LANE : 2 * LANE] = jnp.zeros((chan, LANE), BF16)
-        full[:, LANE:hd] = raw_w[:, LANE:hd] * jnp.asarray(scale, BF16)
-        for k in range(3):
-            full[:, (2 + k) * LANE : (3 + k) * LANE] = dot(
-                raw_p[...], perm(pq3, k, pqh, 2)
-            ).astype(BF16)
-
-    def v_pick(k):
-        a = iota((hd, LANE), 0)
-        b = iota((hd, LANE), 1)
-        start = 2 * vtail if k == 3 else (k - 1) * vtail - pvh
-        return ((a == b + start) & ((b >= pvh) | (k == 3))).astype(BF16)
-
-    for k in range(4):
-        acc = jnp.zeros((chan, LANE), F32)
-        if k < 3:
-            acc = acc + dot(wvpr[...], perm(pv3, k, pvh, 1))
-        if k > 0:
-            acc = acc + dot(wvr[...], v_pick(k))
-        wv[:, k * LANE : (k + 1) * LANE] = acc.astype(BF16)
+    wq[...] = jnp.transpose(wqt[...])
+    wk[...] = jnp.transpose(wkt[...])
+    wv[...] = jnp.transpose(wvt[...])
 
     pw16 = jnp.concatenate([pw_ref[...].astype(F32), jnp.zeros((HP - heads, LANE), F32)], axis=0)
     pw16 = pw16.astype(BF16)
@@ -478,8 +478,10 @@
         vh[:, 3 * LANE : 4 * LANE] = parts[3].astype(BF16)
 
     def query_phase(layer):
+        scale = dh ** -0.5
         message = qx[layer].reshape(nq, chan + LANE)
         fb = dot(message[:, chan:], dec[...])
+        fq[...] = fb
         projected = dot(message[:, :chan], wq[...])
         lane = iota((nq, LANE), 1)
         g = global_points(*tiles(projected, 2, 3), fb)
@@ -489,10 +491,10 @@
         qq = jnp.where(lane < qq0 + heads, hi, qq - hi)
         tail = jnp.where(
             lane < q_tail,
-            projected[:, LANE : 2 * LANE],
+            projected[:, LANE : 2 * LANE] * scale,
             jnp.where(lane < kk0, qq, jnp.where(lane < kk1, 1.0, 0.0)),
         )
-        qf[:, 0:LANE] = projected[:, 0:LANE].astype(BF16).astype(F32)
+        qf[:, 0:LANE] = projected[:, 0:LANE].astype(BF16).astype(F32) * scale
         qf[:, LANE : 2 * LANE] = tail.astype(BF16).astype(F32)
         for k in range(3):
             scaled = g[k] * w_lane
@@ -500,25 +502,27 @@
             qf[:, (2 + k) * LANE : (3 + k) * LANE] = hi
             qf[:, (5 + k) * LANE : (6 + k) * LANE] = jnp.where(lane < pqh, scaled - hi, 0.0)
 
-    group = 2 * rows
-
-    def score_phase(layer):
-        def step(j, carry):
-            parts = []
-            for r in range(group):
-                row = qf[pl.ds(j * group + r, 1), :]
-                parts.append((jnp.broadcast_to(row, (HP, 8 * LANE)) * mh[...]).astype(BF16))
-            s = dot_nt(jnp.concatenate(parts, axis=0), kf[...])
-            for r in range(group):
-                match = jnp.broadcast_to(same[pl.ds(j * group + r, 1), :], (HP, nk))
-                value = s[r * HP : (r + 1) * HP, :] * LOGIT_WEIGHT + match * cw_col + pad_row
-                start = pl.multiple_of((j * group + r) * HP, HP)
-                if layer > 0:
-                    value = value + bias[pl.ds(start, HP), :]
-                scores[pl.ds(start, HP), :] = value
+    def score_chunk(n):
+        parts = []
+        for r in range(rows):
+            row = qf[pl.ds(n * rows + r, 1), :]
+            parts.append((jnp.broadcast_to(row, (HP, 8 * LANE)) * mh[...]).astype(BF16))
+        s = dot_nt(jnp.concatenate(parts, axis=0), kf[...]) * LOGIT_WEIGHT
+        extra = []
+        for r in range(rows):
+            match = jnp.broadcast_to(same[pl.ds(n * rows + r, 1), :], (HP, nk))
+            extra.append(match * cw_col + pad_row)
+        return s + jnp.concatenate(extra, axis=0)
+
+    def chunk_rows(n):
+        return pl.ds(pl.multiple_of(n * rows * HP, rows * HP), rows * HP)
+
+    def score_phase():
+        def step(n, carry):
+            scores[chunk_rows(n), :] = score_chunk(n)
             return carry
 
-        lax.fori_loop(0, nq // group, step, 0)
+        lax.fori_loop(0, nb, step, 0)
 
     def p_copy(layer, n):
         return pltpu.make_async_remote_copy(
@@ -530,135 +534,137 @@
             device_id_type=pl.DeviceIdType.MESH,
         )
 
-    def s_copy(layer, n):
-        return pltpu.make_async_remote_copy(
-            src_ref=ssb.at[layer, n],
-            dst_ref=sr.at[layer, zb],
-            send_sem=s_send.at[layer],
-            recv_sem=s_recv.at[layer, zb],
-            device_id=far_dev(n),
-            device_id_type=pl.DeviceIdType.MESH,
-        )
+    lane_all = iota((rows * HP, LANE), 1)
 
     def chunk_phase(layer):
         def chunk(t):
             n = far_step(t)
             if layer == 0:
-                pltpu.make_async_copy(tile.at[n], tile.at[n], a2a_recv.at[n]).wait()
-            weights = []
-            inverses = []
-            sums = []
-            for r in range(rows):
-                start = pl.multiple_of((n * rows + r) * HP, HP)
-                logits = scores[pl.ds(start, HP), :]
-                pair_rows = tile[n, r]
-                if layer == 0:
-                    own_bias = dot_nt(pw16, pair_rows) * LOGIT_WEIGHT
-                    bias[pl.ds(start, HP), :] = own_bias
-                    logits = logits + own_bias
-                top = jnp.max(logits, axis=1, keepdims=True)
-                p = jnp.exp(logits - top)
-                count = jnp.sum(p, axis=1, keepdims=True)
-                p = p.astype(BF16)
-                inverse = 1.0 / count
-                po[r * HP : (r + 1) * HP, :] = dot(p, pair_rows) * inverse
-                weights.append(p)
-                inverses.append(inverse)
-                sums.append(top + jnp.log(count))
-            p_all = jnp.concatenate(weights, axis=0)
-            main = dot(p_all, vh[...])
-            rest = dot(p_all, vl[...])
-            for r in range(rows):
-                low = r * HP
-                for k in range(4):
-                    value = main[low : low + HP, k * LANE : (k + 1) * LANE]
-                    if k < 3:
-                        value = value + rest[low : low + HP, k * LANE : (k + 1) * LANE]
-                    value = value * inverses[r]
-                    if k == 0:
-                        value = jnp.where(lane_hp < pvh, value, sums[r])
-                    value = value * me_mask[:, k * LANE : (k + 1) * LANE]
-                    ssb[layer, n, r : r + 1, k * LANE : (k + 1) * LANE] = jnp.sum(
-                        value, axis=0, keepdims=True
+                logits = scores[chunk_rows(n), :]
+                with jax.named_scope("tile_wait"):
+                    pltpu.make_async_copy(tile.at[n], tile.at[n], a2a_recv.at[n]).wait()
+                pair_rows = [tile[n, r] for r in range(rows)]
+                own = jnp.concatenate([dot_nt(pw16, v) for v in pair_rows], axis=0) * LOGIT_WEIGHT
+                logits = logits + own
+            else:
+                pair_rows = [tile[n, r] for r in range(rows)]
+                logits = score_chunk(n) + bias[chunk_rows(n), :]
+            top = jnp.max(logits, axis=1, keepdims=True)
+            p = jnp.exp(logits - top)
+            count = jnp.sum(p, axis=1, keepdims=True)
+            p = p.astype(BF16)
+            inverse = 1.0 / count
+            log_sum = top + jnp.log(count)
+            mixed = jnp.concatenate(
+                [dot(p[r * HP : (r + 1) * HP, :], pair_rows[r]) for r in range(rows)], axis=0
+            )
+            main = dot(p, vh[...])
+            rest = dot(p, vl[...])
+            turn = fq[pl.ds(n * rows, rows), :]
+            po[...] = mixed * inverse
+            if layer == 0:
+                bias[chunk_rows(n), :] = own
+            for k in range(4):
+                value = main[:, k * LANE : (k + 1) * LANE]
+                if k < 3:
+                    value = value + rest[:, k * LANE : (k + 1) * LANE]
+                value = value * inverse
+                if k == 0:
+                    value = jnp.where(lane_all < pvh, value, log_sum)
+                for r in range(rows):
+                    sm[r : r + 1, k * LANE : (k + 1) * LANE] = jnp.sum(
+                        value[r * HP : (r + 1) * HP, :]
+                        * me_mask[:, k * LANE : (k + 1) * LANE],
+                        axis=0,
+                        keepdims=True,
                     )
+            part = tiles(sm[...], 0, 4)
+            frame = tiles(turn, 0, 12)
+            moved = [part[k] - frame[9 + k] for k in range(3)]
+            inside = lane8 < pvh
+            for k in range(3):
+                local = frame[k] * moved[0] + frame[3 + k] * moved[1] + frame[6 + k] * moved[2]
+                if k == 0:
+                    hi = part[0].astype(BF16).astype(F32)
+                    other = jnp.where(lane8 < pvh + heads, hi, part[0] - hi)
+                else:
+                    other = part[k]
+                spb[layer, n, heads + k] = jnp.where(inside, local, other).astype(BF16)
+            spb[layer, n, heads + 3] = part[3].astype(BF16)
             for h in range(heads):
                 spb[layer, n, h] = po[pl.ds(h, rows, stride=HP), :].astype(BF16)
             return n
 
         def step(t, carry):
-            n = chunk(t)
-            p_copy(layer, n).start()
-            s_copy(layer, n).start()
+            p_copy(layer, chunk(t)).start()
             return carry
 
         lax.fori_loop(0, nb - 1, step, 0)
         chunk(nb - 1)
 
-    valid = (lane8 >= pvh) & (lane8 < pvh + heads)
-
     def combine(layer):
-        small = [ssb[layer, zb]]
-        slots = [zb]
-        for d in range(1, nb):
-            n = (zb + d) % nb
-            slots.append(n)
-            pltpu.make_async_copy(
-                sr.at[layer, n], sr.at[layer, n], s_recv.at[layer, n]
-            ).wait()
-            small.append(sr[layer, n])
-        sums = [jnp.where(valid, value[:, 0:LANE], 0.0) for value in small]
+        slots = [(zb + d) % nb for d in range(nb)]
+        with jax.named_scope("part_wait"):
+            for n in slots[1:]:
+                pltpu.make_async_copy(pr.at[layer, n], pr.at[layer, n], p_recv.at[layer, n]).wait()
+
+        def piece(d, k):
+            ref = spb if d == 0 else pr
+            return ref[layer, slots[d], k].astype(F32)
+
+        first = jnp.concatenate([piece(d, heads) for d in range(nb)], axis=0)
+        sums = first + pltpu.roll(first, LANE - heads, 1)
+        valid_all = (iota((nb * rows, LANE), 1) >= pvh) & (
+            iota((nb * rows, LANE), 1) < pvh + heads
+        )
+        sums = jnp.where(valid_all, sums, 0.0)
+        valid = (lane8 >= pvh) & (lane8 < pvh + heads)
+        sums = [sums[d * rows : (d + 1) * rows, :] for d in range(nb)]
         top = functools.reduce(jnp.maximum, sums)
         shares = [jnp.where(valid, jnp.exp(value - top), 0.0) for value in sums]
         whole = jnp.where(valid, functools.reduce(jnp.add, shares), 1.0)
         shares = [value / whole for value in shares]
         wide = spread(jnp.concatenate(shares, axis=0), expm[...])
-        mixed = functools.reduce(
-            jnp.add, [wide[d * rows : (d + 1) * rows, :] * small[d] for d in range(nb)]
-        )
-        for d in range(1, nb):
-            pltpu.make_async_copy(
-                pr.at[layer, slots[d]], pr.at[layer, slots[d]], p_recv.at[layer, slots[d]]
-            ).wait()
+        mixed = []
+        for k in range(4):
+            acc = None
+            for d in range(nb):
+                term = wide[d * rows : (d + 1) * rows, k * LANE : (k + 1) * LANE] * piece(
+                    d, heads + k
+                )
+                acc = term if acc is None else acc + term
+            mixed.append(acc)
         pairs = []
         for h in range(heads):
             acc = None
             for d in range(nb):
-                part = spb[layer, zb, h] if d == 0 else pr[layer, slots[d], h]
-                term = col(shares[d], pvh + h) * part.astype(F32)
+                term = col(shares[d], pvh + h) * piece(d, h)
                 acc = term if acc is None else acc + term
             pairs.append(acc)
         return mixed, pairs
 
+    def gain_row(ref):
+        return jnp.concatenate([ref[k : k + 1, :] for k in range(chan // LANE)], axis=1)
+
     def update(layer, state, fr, mixed, pairs):
         turn = [col(fr, k) for k in range(9)]
         shift = [col(fr, 9 + k) for k in range(3)]
-        mix = tiles(mixed, 0, 4)
-        moved = [mix[k] - shift[k] for k in range(3)]
-        local = [
-            turn[k] * moved[0] + turn[3 + k] * moved[1] + turn[6 + k] * moved[2] for k in range(3)
-        ]
         inside = lane8 < pvh
         norm = jnp.sqrt(
-            local[0] * local[0] + local[1] * local[1] + local[2] * local[2] + 1e-08
-        )
-        concat = [
-            jnp.where(inside, local[0], 0.0),
-            jnp.where(inside, local[1], mix[1]),
-            jnp.where(inside, local[2], mix[2]),
-            mix[3],
-            jnp.where(inside, norm, 0.0),
-        ] + pairs
+            mixed[0] * mixed[0] + mixed[1] * mixed[1] + mixed[2] * mixed[2] + 1e-08
+        )
+        concat = mixed + [jnp.where(inside, norm, 0.0)] + pairs
         concat = jnp.concatenate(concat, axis=1).astype(BF16)
         if layer == 0:
             for copy in wo_copies:
                 copy.wait()
         state = state + dot(concat, wo[...])
-        normed = layer_norm(state, g1_ref[...])
+        normed = layer_norm(state, gain_row(g1_ref))
         hidden = jnp.maximum(dot(normed.astype(BF16), m1[...]), 0.0).astype(BF16)
         hidden = jnp.maximum(dot(hidden, m2[...]), 0.0).astype(BF16)
-        state = layer_norm(normed + dot(hidden, m3[...]), g2_ref[...])
+        state = layer_norm(normed + dot(hidden, m3[...]), gain_row(g2_ref))
         state_bf = state.astype(BF16)
-        upd = dot(state_bf, fw_ref[...])
+        upd = dot_nt(state_bf, fw_ref[...])
         u = [jnp.broadcast_to(upd[:, k : k + 1], (rows, LANE)) for k in range(6)]
         inverse = lax.rsqrt(1.0 + u[0] * u[0] + u[1] * u[1] + u[2] * u[2])
         vx, vy, vz = u[0] * inverse, u[1] * inverse, u[2] * inverse
@@ -697,23 +703,38 @@
 
     state = single[...].astype(F32)
     for layer in range(LAYERS):
-        pltpu.make_async_copy(
-            kx.at[layer, 0 : g_count - 1], kx.at[layer, 0 : g_count - 1], kx_recv.at[layer]
-        ).wait()
-        key_phase(layer)
-        pltpu.make_async_copy(
-            qx.at[layer, 0 : nb - 1], qx.at[layer, 0 : nb - 1], qx_recv.at[layer]
-        ).wait()
-        query_phase(layer)
-        score_phase(layer)
-        chunk_phase(layer)
-        mixed, pairs = combine(layer)
-        state, state_bf, frames = update(layer, state, frames, mixed, pairs)
+        with jax.named_scope(f"key_wait_{layer}"):
+            pltpu.make_async_copy(
+                kx.at[layer, 0 : g_count - 1], kx.at[layer, 0 : g_count - 1], kx_recv.at[layer]
+            ).wait()
+        with jax.named_scope(f"key_{layer}"):
+            key_phase(layer)
+        with jax.named_scope(f"query_wait_{layer}"):
+            pltpu.make_async_copy(
+                qx.at[layer, 0 : nb - 1], qx.at[layer, 0 : nb - 1], qx_recv.at[layer]
+            ).wait()
+        with jax.named_scope(f"query_{layer}"):
+            query_phase(layer)
+        if layer == 0:
+            with jax.named_scope(f"score_{layer}"):
+                score_phase()
+        with jax.named_scope(f"chunk_{layer}"):
+            chunk_phase(layer)
+        with jax.named_scope(f"combine_{layer}"):
+            mixed, pairs = combine(layer)
+        with jax.named_scope(f"update_{layer}"):
+            state, state_bf, frames = update(layer, state, frames, mixed, pairs)
         if layer + 1 < LAYERS:
-            put_message(layer + 1, state_bf, frames)
-            send_message(layer + 1)
+            with jax.named_scope(f"send_{layer}"):
+                put_message(layer + 1, state_bf, frames)
+                send_message(layer + 1)
     out_state[...] = state
-    out_frames[...] = frames
+    out_turn[...] = frames[:, 0:9]
+    pick = (iota((3, LANE), 1) == iota((3, LANE), 0) + 9).astype(F32)
+    out_shift[...] = lax.dot_general(
+        pick, frames, (((1,), (1,)), ((), ())), precision=lax.Precision.HIGHEST,
+        preferred_element_type=F32,
+    )
 
     for layer in range(LAYERS):
         pltpu.make_async_copy(
@@ -725,12 +746,8 @@
         pltpu.make_async_copy(
             pr.at[layer, 0 : nb - 1], pr.at[layer, 0 : nb - 1], p_send.at[layer]
         ).wait()
-        pltpu.make_async_copy(
-            sr.at[layer, 0 : nb - 1], sr.at[layer, 0 : nb - 1], s_send.at[layer]
-        ).wait()
     for offset in near:
-        px, pzp, pc = near_id(offset)
-        pltpu.make_async_copy(pair.at[px, :, pzp, pc], pair.at[px, :, pzp, pc], a2a_send).wait()
+        pltpu.make_async_copy(pair.at[0, :, 0, 0], pair.at[0, :, 0, 0], a2a_send).wait()
 
 
 def on_device(
@@ -777,12 +794,9 @@
         pltpu.VMEM((LAYERS, g_count, rows, width), BF16),
         pltpu.VMEM((LAYERS, nb, rows, width), BF16),
         pltpu.VMEM((LAYERS, rows, width), BF16),
-        pltpu.VMEM(query_weight.shape, BF16),
-        pltpu.VMEM(key_weight.shape, BF16),
-        pltpu.VMEM(value_weight.shape, BF16),
-        pltpu.VMEM(qpoint_weight.shape, BF16),
-        pltpu.VMEM(kpoint_weight.shape, BF16),
-        pltpu.VMEM(vpoint_weight.shape, BF16),
+        pltpu.VMEM((5 * LANE, chan), BF16),
+        pltpu.VMEM((5 * LANE, chan), BF16),
+        pltpu.VMEM((4 * LANE, chan), BF16),
         pltpu.VMEM((chan, 5 * LANE), BF16),
         pltpu.VMEM((chan, 5 * LANE), BF16),
         pltpu.VMEM((chan, 4 * LANE), BF16),
@@ -802,11 +816,11 @@
         pltpu.VMEM((HP, 8 * LANE), F32),
         pltpu.VMEM((HP, 4 * LANE), F32),
         pltpu.VMEM((rows * HP, LANE), F32),
-        pltpu.VMEM((LAYERS, nb, heads, rows, LANE), BF16),
-        pltpu.VMEM((LAYERS, nb, rows, 4 * LANE), F32),
-        pltpu.VMEM((LAYERS, nb, heads, rows, LANE), BF16),
-        pltpu.VMEM((LAYERS, nb, rows, 4 * LANE), F32),
-        pltpu.SemaphoreType.DMA((9,)),
+        pltpu.VMEM((rows, 4 * LANE), F32),
+        pltpu.VMEM((nq, 12 * LANE), F32),
+        pltpu.VMEM((LAYERS, nb, heads + 4, rows, LANE), BF16),
+        pltpu.VMEM((LAYERS, nb, heads + 4, rows, LANE), BF16),
+        pltpu.SemaphoreType.DMA((23,)),
         pltpu.SemaphoreType.DMA((8,)),
         pltpu.SemaphoreType.DMA((nb,)),
         pltpu.SemaphoreType.DMA,
@@ -814,48 +828,47 @@
         pltpu.SemaphoreType.DMA((LAYERS,)),
         pltpu.SemaphoreType.DMA((LAYERS,)),
         pltpu.SemaphoreType.DMA((LAYERS,)),
-        pltpu.SemaphoreType.DMA((LAYERS,)),
-        pltpu.SemaphoreType.DMA((LAYERS, nb)),
         pltpu.SemaphoreType.DMA((LAYERS, nb)),
     ]
-    state, frames = pl.pallas_call(
+    state, turned, moved = pl.pallas_call(
         functools.partial(kernel, (nx, nb, cores, rows, heads)),
         name="structure_layers",
         out_shape=(
             jax.ShapeDtypeStruct((rows, chan), F32),
-            jax.ShapeDtypeStruct((rows, LANE), F32),
+            jax.ShapeDtypeStruct((rows, 9), F32),
+            jax.ShapeDtypeStruct((3, rows), F32),
         ),
         in_specs=in_specs,
-        out_specs=(vmem, vmem),
+        out_specs=(vmem, vmem, vmem),
         scratch_shapes=scratch,
         compiler_params=pltpu.CompilerParams(
-            collective_id=0, has_side_effects=True, vmem_limit_bytes=48 * 1024 * 1024
+            collective_id=0, has_side_effects=True, vmem_limit_bytes=62 * 1024 * 1024
         ),
     )(
         pair,
         single,
-        rotation,
+        jnp.transpose(rotation),
         translation,
         residue_mask.reshape(-1, LANE),
         chain_index.reshape(-1, LANE),
-        query_weight,
-        key_weight,
-        value_weight,
-        qpoint_weight,
-        kpoint_weight,
-        vpoint_weight,
+        jnp.transpose(query_weight),
+        jnp.transpose(key_weight),
+        jnp.transpose(value_weight),
+        jnp.transpose(qpoint_weight),
+        jnp.transpose(kpoint_weight),
+        jnp.transpose(vpoint_weight),
         pair_weight,
         head_weight.reshape(1, -1),
         chain_weight.reshape(1, -1),
         output_weight,
-        gain_first.reshape(1, -1),
+        gain_first.reshape(-1, LANE),
         mlp_first,
         mlp_second,
         mlp_third,
-        gain_second.reshape(1, -1),
-        frame_weight,
+        gain_second.reshape(-1, LANE),
+        jnp.transpose(frame_weight),
     )
-    return state, jnp.transpose(frames[:, :9]), jnp.transpose(frames[:, 9:12])
+    return state, jnp.transpose(turned), moved
 
 
 def solution(mesh):

time: 117 us -> 91.3 us (0.78)
  Pallas kernels: 99.5 us -> 86.1 us
  local copies, waits for them, and re-layouts: 15.8 us -> 3.82 us
    pallas_call x1, Pallas kernels: 99.5 us -> 86.1 us  [on_device(): pl.pallas_call(functools.partial(kernel, (nx, nb, cores, rows, heads)), n...]
    unnamed x34 -> x3, local copies, waits for them, and re-layouts: 13.6 us -> 3.82 us
    reshape x2 -> x0, local copies, waits for them, and re-layouts: 1.52 us -> none  [the longest x1 0.83 us: on_device(): gain_first.reshape(1, -1)]
where the time goes in v2:
time: 91.3 us; the launch traced here: 90.6 us
  Pallas kernels  86.1 us (94%)
  local copies, waits for them, and re-layouts  3.82 us (4%)
    pallas_call x1, Pallas kernels, on_device(): pl.pallas_call(functools.partial(kernel, (nx, nb, cores, rows, heads)), n...  86.1 us
    unnamed x3, local copies, waits for them, and re-layouts  3.82 us

profile of v2, /device:TPU:33, one launch (start us, length us, event | category | flops | bytes accessed | tf_op | source)
XLA Modules:
  0.0 90.6 jit_solution(12853764924028428318)
XLA Ops:
  0.6 86.1 %structure_layers.1 = (f32[8,384]{1,0:T(8,128)}, f32[8,9]{1,0:T(8,128)}, f32[3,8]{1,0:T(4,128)}) custom-call(bf16[4,8,2,2,8,8,128]{6,5,4,3,2,1,0:T(8,128)(2,1)} %bitcast.16, bf16[8,384]{1,0:T(8,128)(2,1)} %single.1, f32[8,9]{1,0:T(8,128)} %bitcast.25, f32[3,8]{1,0:T(4,128)} %translation.1, s32[8,128]{1,0:T(8,128)} %bitcast.26, s32[8,128]{1,0:T(8,128)} %bitcast.27, ...), custom_call_target="tpu_custom_call" | custom-call | tf_op jit(solution)/shard_map/structure_layers/pallas_call | solution.py:833
  86.8 1.3 %copy.28 = f32[8,384]{1,0:T(8,128)} copy(f32[8,384]{1,0:T(8,128)} %get-tuple-element.12) | data formatting | bytes 24576
  88.1 1.3 %copy.29 = f32[9,8]{0,1:T(8,128)} copy(f32[9,8]{0,1:T(8,128)} %bitcast.24) | data formatting | bytes 576
  89.3 1.2 %copy.30 = f32[3,8]{1,0:T(4,128)} copy(f32[3,8]{1,0:T(4,128)} %get-tuple-element.14) | data formatting | bytes 192

commit v3 on v2

--- a/solution.py
+++ b/solution.py
@@ -60,30 +60,41 @@
 def kernel(
     sizes,
     pair,
-    single,
-    rotation,
-    translation,
-    mask,
-    chain,
+    single_hbm,
+    rotation_hbm,
+    translation_hbm,
+    mask_hbm,
+    chain_hbm,
     wq_hbm,
     wk_hbm,
     wv_hbm,
     wqp_hbm,
     wkp_hbm,
     wvp_hbm,
+    pw_hbm,
+    hw_hbm,
+    cw_hbm,
+    wo_hbm,
+    g1_hbm,
+    m1_hbm,
+    m2_hbm,
+    m3_hbm,
+    g2_hbm,
+    fw_hbm,
+    out_state,
+    out_turn,
+    out_shift,
+    single,
+    rotation,
+    translation,
+    mask,
+    chain,
     pw_ref,
     hw_ref,
     cw_ref,
-    wo_hbm,
     g1_ref,
-    m1_hbm,
-    m2_hbm,
-    m3_hbm,
     g2_ref,
     fw_ref,
-    out_state,
-    out_turn,
-    out_shift,
     tile,
     kx,
     qx,
@@ -114,6 +125,11 @@
     fq,
     spb,
     pr,
+    state_buf,
+    turn_buf,
+    shift_buf,
+    last_sem,
+    small_sem,
     w_sem,
     wo_sem,
     a2a_recv,
@@ -191,7 +207,124 @@
             device_id=dev(*source_id(offset)),
             device_id_type=pl.DeviceIdType.MESH,
         )
-
+    small = [
+        (single_hbm, single),
+        (rotation_hbm, rotation),
+        (translation_hbm, translation),
+        (mask_hbm, mask),
+        (chain_hbm, chain),
+        (pw_hbm, pw_ref),
+        (hw_hbm, hw_ref),
+        (cw_hbm, cw_ref),
+        (g1_hbm, g1_ref),
+        (g2_hbm, g2_ref),
+        (fw_hbm, fw_ref),
+    ]
+    small_copies = [
+        pltpu.make_async_copy(src, dst, small_sem.at[k]) for k, (src, dst) in enumerate(small)
+    ]
+    for copy in small_copies:
+        copy.start()
+
+    across = [offset for offset in near if offset[1]]
+    within = [offset for offset in near if not offset[1]]
+
+    def exchange(t, offsets):
+        n = far_step(t)
+        for offset in offsets:
+            px, pz, pc = near_id(offset)
+            pltpu.make_async_remote_copy(
+                src_ref=pair.at[px, n, pz % SPAN, pc],
+                dst_ref=tile.at[n, :, pl.ds(place(pc) * rows, rows), :],
+                send_sem=a2a_send,
+                recv_sem=a2a_recv.at[n],
+                device_id=dev(px, pz, pc),
+                device_id_type=pl.DeviceIdType.MESH,
+            ).start()
+
+    def exchange_across(t, carry):
+        exchange(t, across)
+        return carry
+
+    def exchange_within(t, carry):
+        n = far_step(t)
+        exchange(t, within)
+        pltpu.make_async_copy(
+            pair.at[x, n, zp, c], tile.at[n, :, pl.ds(me * rows, rows), :], a2a_recv.at[n]
+        ).start()
+        return carry
+
+    first = min(2, nb)
+
+    with jax.named_scope("barrier"):
+        pl.semaphore_wait(barrier, len(near) + nb - 1)
+    exchange_across(0, 0)
+    exchange_within(0, 0)
+
+    lane8 = iota((rows, LANE), 1)
+    for copy in small_copies[:3]:
+        copy.wait()
+    take_r = (
+        (iota((9, LANE), 1) % 12 == iota((9, LANE), 0)) & (iota((9, LANE), 1) < 36)
+    ).astype(F32)
+    take_t = (
+        (iota((3, LANE), 1) % 12 == iota((3, LANE), 0) + 9) & (iota((3, LANE), 1) < 36)
+    ).astype(F32)
+    contract0 = (((0,), (0,)), ((), ()))
+    frames = jnp.dot(
+        rotation[...], take_r, precision=lax.Precision.HIGHEST, preferred_element_type=F32
+    ) + lax.dot_general(
+        translation[...], take_t, contract0, precision=lax.Precision.HIGHEST,
+        preferred_element_type=F32,
+    )
+
+    def frame_columns(fr):
+        hi = fr.astype(BF16).astype(F32)
+        mid = (fr - hi).astype(BF16).astype(F32)
+        lo = fr - hi - mid
+        return jnp.where(lane8 < 12, hi, jnp.where(lane8 < 24, mid, lo)).astype(BF16)
+
+    def put_message(layer, state_bf, fr):
+        tail = frame_columns(fr)
+        for ref in (xs.at[layer], kx.at[layer, me], qx.at[layer, zb]):
+            ref[:, 0:chan] = state_bf
+            ref[:, chan : chan + LANE] = tail
+
+    def x_near(layer, offset):
+        target = near_id(offset)
+        return pltpu.make_async_remote_copy(
+            src_ref=xs.at[layer],
+            dst_ref=kx.at[layer, place(target[2])],
+            send_sem=x_send.at[layer],
+            recv_sem=kx_recv.at[layer],
+            device_id=dev(*target),
+            device_id_type=pl.DeviceIdType.MESH,
+        )
+
+    def far_copy(layer, block):
+        return pltpu.make_async_remote_copy(
+            src_ref=xs.at[layer],
+            dst_ref=qx.at[layer, zb],
+            send_sem=x_send.at[layer],
+            recv_sem=qx_recv.at[layer],
+            device_id=far_dev(block),
+            device_id_type=pl.DeviceIdType.MESH,
+        )
+
+    def send_message(layer):
+        for t in range(nb - 1):
+            far_copy(layer, far_step(t)).start()
+        for offset in near:
+            x_near(layer, offset).start()
+
+    put_message(0, single[...], frames)
+    send_message(0)
+    with jax.named_scope("exchange"):
+        for t in range(1, first):
+            exchange_across(t, 0)
+            exchange_within(t, 0)
+        lax.fori_loop(first, nb, exchange_across, 0)
+        lax.fori_loop(first, nb, exchange_within, 0)
     moves = [(wq_hbm, 0, wqt, 0, hd), (wk_hbm, 0, wkt, 0, hd)]
     for src, dst in ((wqp_hbm, wqt), (wkp_hbm, wkt)):
         for k in range(3):
@@ -246,85 +379,9 @@
     for copy in wo_copies:
         copy.start()
 
-    lane8 = iota((rows, LANE), 1)
-    take_r = (
-        (iota((9, LANE), 1) % 12 == iota((9, LANE), 0)) & (iota((9, LANE), 1) < 36)
-    ).astype(F32)
-    take_t = (
-        (iota((3, LANE), 1) % 12 == iota((3, LANE), 0) + 9) & (iota((3, LANE), 1) < 36)
-    ).astype(F32)
-    contract0 = (((0,), (0,)), ((), ()))
-    frames = jnp.dot(
-        rotation[...], take_r, precision=lax.Precision.HIGHEST, preferred_element_type=F32
-    ) + lax.dot_general(
-        translation[...], take_t, contract0, precision=lax.Precision.HIGHEST,
-        preferred_element_type=F32,
-    )
-
-    def frame_columns(fr):
-        hi = fr.astype(BF16).astype(F32)
-        mid = (fr - hi).astype(BF16).astype(F32)
-        lo = fr - hi - mid
-        return jnp.where(lane8 < 12, hi, jnp.where(lane8 < 24, mid, lo)).astype(BF16)
-
-    def put_message(layer, state_bf, fr):
-        tail = frame_columns(fr)
-        for ref in (xs.at[layer], kx.at[layer, me], qx.at[layer, zb]):
-            ref[:, 0:chan] = state_bf
-            ref[:, chan : chan + LANE] = tail
-
-    def x_near(layer, offset):
-        target = near_id(offset)
-        return pltpu.make_async_remote_copy(
-            src_ref=xs.at[layer],
-            dst_ref=kx.at[layer, place(target[2])],
-            send_sem=x_send.at[layer],
-            recv_sem=kx_recv.at[layer],
-            device_id=dev(*target),
-            device_id_type=pl.DeviceIdType.MESH,
-        )
-
-    def x_far(layer, t):
-        return pltpu.make_async_remote_copy(
-            src_ref=xs.at[layer],
-            dst_ref=qx.at[layer, zb],
-            send_sem=x_send.at[layer],
-            recv_sem=qx_recv.at[layer],
-            device_id=far_dev(far_step(t)),
-            device_id_type=pl.DeviceIdType.MESH,
-        )
-
-    def send_message(layer):
-        for t in range(nb - 1):
-            x_far(layer, t).start()
-        for offset in near:
-            x_near(layer, offset).start()
-
-    put_message(0, single[...], frames)
-    with jax.named_scope("barrier"):
-        pl.semaphore_wait(barrier, len(near) + nb - 1)
-    send_message(0)
-
-    def a2a_step(t, carry):
-        n = far_step(t)
-        for offset in near:
-            px, pz, pc = near_id(offset)
-            pltpu.make_async_remote_copy(
-                src_ref=pair.at[px, n, pz % SPAN, pc],
-                dst_ref=tile.at[n, :, pl.ds(place(pc) * rows, rows), :],
-                send_sem=a2a_send,
-                recv_sem=a2a_recv.at[n],
-                device_id=dev(px, pz, pc),
-                device_id_type=pl.DeviceIdType.MESH,
-            ).start()
-        pltpu.make_async_copy(
-            pair.at[x, n, zp, c], tile.at[n, :, pl.ds(me * rows, rows), :], a2a_recv.at[n]
-        ).start()
-        return carry
-
-    with jax.named_scope("exchange"):
-        lax.fori_loop(0, nb, a2a_step, 0)
-
+
+    for copy in small_copies[3:]:
+        copy.wait()
     lane_row = iota((1, LANE), 1)
 
     def as_col(row):
@@ -663,6 +720,9 @@
         hidden = jnp.maximum(dot(normed.astype(BF16), m1[...]), 0.0).astype(BF16)
         hidden = jnp.maximum(dot(hidden, m2[...]), 0.0).astype(BF16)
         state = layer_norm(normed + dot(hidden, m3[...]), gain_row(g2_ref))
+        if layer == LAYERS - 1:
+            state_buf[...] = state
+            last_copies[0].start()
         state_bf = state.astype(BF16)
         upd = dot_nt(state_bf, fw_ref[...])
         u = [jnp.broadcast_to(upd[:, k : k + 1], (rows, LANE)) for k in range(6)]
@@ -701,6 +761,12 @@
             fr = jnp.where((lane8 % 12 == k) & (lane8 < 36), entries[k], fr)
         return state, state_bf, fr
 
+    last_copies = [
+        pltpu.make_async_copy(src, dst, last_sem.at[k])
+        for k, (src, dst) in enumerate(
+            ((state_buf, out_state), (turn_buf, out_turn), (shift_buf, out_shift))
+        )
+    ]
     state = single[...].astype(F32)
     for layer in range(LAYERS):
         with jax.named_scope(f"key_wait_{layer}"):
@@ -728,14 +794,14 @@
             with jax.named_scope(f"send_{layer}"):
                 put_message(layer + 1, state_bf, frames)
                 send_message(layer + 1)
-    out_state[...] = state
-    out_turn[...] = frames[:, 0:9]
+    turn_buf[...] = frames[:, 0:9]
     pick = (iota((3, LANE), 1) == iota((3, LANE), 0) + 9).astype(F32)
-    out_shift[...] = lax.dot_general(
+    shift_buf[...] = lax.dot_general(
         pick, frames, (((1,), (1,)), ((), ())), precision=lax.Precision.HIGHEST,
         preferred_element_type=F32,
     )
-
+    last_copies[1].start()
+    last_copies[2].start()
     for layer in range(LAYERS):
         pltpu.make_async_copy(
             kx.at[layer, 0 : g_count - 1], kx.at[layer, 0 : g_count - 1], x_send.at[layer]
@@ -748,6 +814,19 @@
         ).wait()
     for offset in near:
         pltpu.make_async_copy(pair.at[0, :, 0, 0], pair.at[0, :, 0, 0], a2a_send).wait()
+    for copy in last_copies:
+        copy.wait()
+
+
+def hand_over(a, b, c, a_out, b_out, c_out, sem):
+    copies = [
+        pltpu.make_async_copy(src, dst, sem.at[k])
+        for k, (src, dst) in enumerate(((a, a_out), (b, b_out), (c, c_out)))
+    ]
+    for copy in copies:
+        copy.start()
+    for copy in copies:
+        copy.wait()
 
 
 def on_device(
@@ -786,10 +865,21 @@
     nq = nb * rows
     width = chan + LANE
     pair = pair_cols.reshape(nx, nb, SPAN, cores, rows, *pair_cols.shape[1:])
-    vmem = pl.BlockSpec(memory_space=pltpu.VMEM)
     hbm = pl.BlockSpec(memory_space=pl.ANY)
-    in_specs = [hbm] + [vmem] * 5 + [hbm] * 6 + [vmem] * 3 + [hbm, vmem] + [hbm] * 3 + [vmem] * 2
-    scratch = [
+    small = [
+        single,
+        jnp.transpose(rotation),
+        translation,
+        residue_mask.reshape(-1, LANE),
+        chain_index.reshape(-1, LANE),
+        pair_weight,
+        head_weight.reshape(1, -1),
+        chain_weight.reshape(1, -1),
+        gain_first.reshape(-1, LANE),
+        gain_second.reshape(-1, LANE),
+        jnp.transpose(frame_weight),
+    ]
+    scratch = [pltpu.VMEM(v.shape, v.dtype) for v in small] + [
         pltpu.VMEM((nb, rows, nk, LANE), BF16),
         pltpu.VMEM((LAYERS, g_count, rows, width), BF16),
         pltpu.VMEM((LAYERS, nb, rows, width), BF16),
@@ -820,6 +910,11 @@
         pltpu.VMEM((nq, 12 * LANE), F32),
         pltpu.VMEM((LAYERS, nb, heads + 4, rows, LANE), BF16),
         pltpu.VMEM((LAYERS, nb, heads + 4, rows, LANE), BF16),
+        pltpu.VMEM((rows, chan), F32),
+        pltpu.VMEM((rows, 9), F32),
+        pltpu.VMEM((3, rows), F32),
+        pltpu.SemaphoreType.DMA((3,)),
+        pltpu.SemaphoreType.DMA((11,)),
         pltpu.SemaphoreType.DMA((23,)),
         pltpu.SemaphoreType.DMA((8,)),
         pltpu.SemaphoreType.DMA((nb,)),
@@ -838,36 +933,39 @@
             jax.ShapeDtypeStruct((rows, 9), F32),
             jax.ShapeDtypeStruct((3, rows), F32),
         ),
-        in_specs=in_specs,
-        out_specs=(vmem, vmem, vmem),
+        in_specs=[hbm] * 22,
+        out_specs=(hbm, hbm, hbm),
         scratch_shapes=scratch,
         compiler_params=pltpu.CompilerParams(
             collective_id=0, has_side_effects=True, vmem_limit_bytes=62 * 1024 * 1024
         ),
     )(
         pair,
-        single,
-        jnp.transpose(rotation),
-        translation,
-        residue_mask.reshape(-1, LANE),
-        chain_index.reshape(-1, LANE),
+        *small[:5],
         jnp.transpose(query_weight),
         jnp.transpose(key_weight),
         jnp.transpose(value_weight),
         jnp.transpose(qpoint_weight),
         jnp.transpose(kpoint_weight),
         jnp.transpose(vpoint_weight),
-        pair_weight,
-        head_weight.reshape(1, -1),
-        chain_weight.reshape(1, -1),
+        *small[5:8],
         output_weight,
-        gain_first.reshape(-1, LANE),
+        small[8],
         mlp_first,
         mlp_second,
         mlp_third,
-        gain_second.reshape(-1, LANE),
-        jnp.transpose(frame_weight),
+        small[9],
+        small[10],
     )
+    state, turned, moved = pl.pallas_call(
+        hand_over,
+        name="hand_over",
+        out_shape=tuple(jax.ShapeDtypeStruct(v.shape, v.dtype) for v in (state, turned, moved)),
+        in_specs=[hbm] * 3,
+        out_specs=(hbm,) * 3,
+        scratch_shapes=[pltpu.SemaphoreType.DMA((3,))],
+        compiler_params=pltpu.CompilerParams(vmem_limit_bytes=62 * 1024 * 1024),
+    )(state, turned, moved)
     return state, jnp.transpose(turned), moved
 
 

time: 91.3 us -> 89.1 us (0.976)
  local copies, waits for them, and re-layouts: 3.82 us -> 0 us
  Pallas kernels: 86.1 us -> 88.4 us
    unnamed x3 -> x0, local copies, waits for them, and re-layouts: 3.82 us -> none
    pallas_call x0 -> x1, Pallas kernels: none -> 1.67 us  [on_device(): pl.pallas_call(hand_over, name='hand_over', out_shape=tuple((jax.ShapeDty...]
where the time goes in v3:
time: 89.1 us; the launch traced here: 89 us
  Pallas kernels  88.4 us (99%)
    pallas_call x1, Pallas kernels, on_device(): pl.pallas_call(functools.partial(kernel, (nx, nb, cores, rows, heads)), n...  86.7 us

profile of v3, /device:TPU:33, one launch (start us, length us, event | category | flops | bytes accessed | tf_op | source)
XLA Modules:
  0.0 89.0 jit_solution(13588348426073677422)
XLA Ops:
  0.6 86.7 %structure_layers.1 = (f32[8,384]{1,0:T(8,128)}, f32[8,9]{1,0:T(8,128)}, f32[3,8]{1,0:T(4,128)}) custom-call(bf16[4,8,2,2,8,8,128]{6,5,4,3,2,1,0:T(8,128)(2,1)} %bitcast.16, bf16[8,384]{1,0:T(8,128)(2,1)} %single_hbm.1, f32[8,9]{1,0:T(8,128)} %bitcast.24, f32[3,8]{1,0:T(4,128)} %translation_hbm.1, s32[8,128]{1,0:T(8,128)} %bitcast.25, s32[8,128]{1,0:T(8,128)} %bitcast.26, ...), custom_call_target="tpu_custom_call" | custom-call | tf_op jit(solution)/shard_map/structure_layers/pallas_call | solution.py:928
  87.3 1.7 %hand_over.1 = (f32[8,384]{1,0:T(8,128)}, f32[8,9]{1,0:T(8,128)}, f32[3,8]{1,0:T(4,128)}) custom-call(f32[8,384]{1,0:T(8,128)} %get-tuple-element.9.a, f32[8,9]{1,0:T(8,128)} %get-tuple-element.10.b, f32[3,8]{1,0:T(4,128)} %get-tuple-element.11.c), custom_call_target="tpu_custom_call" | custom-call | tf_op jit(solution)/shard_map/hand_over/pallas_call | solution.py:960

commit v4 on v3

--- a/solution.py
+++ b/solution.py
@@ -190,10 +190,10 @@
     def far_dev(block):
         return dev(x, block * SPAN + zp, c)
 
-    def far_step(t):
+    def far_step(t, block=None):
         half = (t + 1) // 2
         sign = 1 - 2 * (t % 2)
-        return (zb + nb // 2 + sign * half + nb) % nb
+        return ((zb if block is None else block) + nb // 2 + sign * half + nb) % nb
 
     barrier = pltpu.get_barrier_semaphore()
     for t in range(nb - 1):
@@ -230,9 +230,9 @@
     within = [offset for offset in near if not offset[1]]
 
     def exchange(t, offsets):
-        n = far_step(t)
         for offset in offsets:
             px, pz, pc = near_id(offset)
+            n = far_step(t, pz // SPAN)
             pltpu.make_async_remote_copy(
                 src_ref=pair.at[px, n, pz % SPAN, pc],
                 dst_ref=tile.at[n, :, pl.ds(place(pc) * rows, rows), :],
@@ -242,24 +242,22 @@
                 device_id_type=pl.DeviceIdType.MESH,
             ).start()
 
-    def exchange_across(t, carry):
-        exchange(t, across)
-        return carry
+    def exchange_across(t):
+        if t < nb:
+            exchange(t, across)
 
     def exchange_within(t, carry):
+        exchange(t, within)
         n = far_step(t)
-        exchange(t, within)
         pltpu.make_async_copy(
             pair.at[x, n, zp, c], tile.at[n, :, pl.ds(me * rows, rows), :], a2a_recv.at[n]
         ).start()
         return carry
 
-    first = min(2, nb)
-
     with jax.named_scope("barrier"):
         pl.semaphore_wait(barrier, len(near) + nb - 1)
-    exchange_across(0, 0)
     exchange_within(0, 0)
+    exchange_across(0)
 
     lane8 = iota((rows, LANE), 1)
     for copy in small_copies[:3]:
@@ -320,11 +318,8 @@
     put_message(0, single[...], frames)
     send_message(0)
     with jax.named_scope("exchange"):
-        for t in range(1, first):
-            exchange_across(t, 0)
-            exchange_within(t, 0)
-        lax.fori_loop(first, nb, exchange_across, 0)
-        lax.fori_loop(first, nb, exchange_within, 0)
+        lax.fori_loop(1, nb, exchange_within, 0)
+        exchange_across(1)
     moves = [(wq_hbm, 0, wqt, 0, hd), (wk_hbm, 0, wkt, 0, hd)]
     for src, dst in ((wqp_hbm, wqt), (wkp_hbm, wkt)):
         for k in range(3):
@@ -597,6 +592,11 @@
         def chunk(t):
             n = far_step(t)
             if layer == 0:
+
+                @pl.when((t >= 2) & (t + 4 < nb))
+                def _():
+                    exchange(t + 4, across)
+
                 logits = scores[chunk_rows(n), :]
                 with jax.named_scope("tile_wait"):
                     pltpu.make_async_copy(tile.at[n], tile.at[n], a2a_recv.at[n]).wait()
@@ -769,10 +769,14 @@
     ]
     state = single[...].astype(F32)
     for layer in range(LAYERS):
+        if layer == 0:
+            exchange_across(2)
         with jax.named_scope(f"key_wait_{layer}"):
             pltpu.make_async_copy(
                 kx.at[layer, 0 : g_count - 1], kx.at[layer, 0 : g_count - 1], kx_recv.at[layer]
             ).wait()
+        if layer == 0:
+            exchange_across(3)
         with jax.named_scope(f"key_{layer}"):
             key_phase(layer)
         with jax.named_scope(f"query_wait_{layer}"):
@@ -782,8 +786,10 @@
         with jax.named_scope(f"query_{layer}"):
             query_phase(layer)
         if layer == 0:
+            exchange_across(4)
             with jax.named_scope(f"score_{layer}"):
                 score_phase()
+            exchange_across(5)
         with jax.named_scope(f"chunk_{layer}"):
             chunk_phase(layer)
         with jax.named_scope(f"combine_{layer}"):

time: 89.1 us -> 87.1 us (0.978); the launches traced: 89 us -> 85.7 us
  Pallas kernels: 88.4 us -> 85 us
    pallas_call x1, Pallas kernels: 86.7 us -> 83.3 us  [on_device(): pl.pallas_call(functools.partial(kernel, (nx, nb, cores, rows, heads)), n...]
where the time goes in v4:
time: 87.1 us; the launch traced here: 85.7 us
  Pallas kernels  85 us (98%)
    pallas_call x1, Pallas kernels, on_device(): pl.pallas_call(functools.partial(kernel, (nx, nb, cores, rows, heads)), n...  83.3 us

profile of v4, /device:TPU:33, one launch (start us, length us, event | category | flops | bytes accessed | tf_op | source)
XLA Modules:
  0.0 85.7 jit_solution(16076606132347386175)
XLA Ops:
  0.6 83.3 %structure_layers.1 = (f32[8,384]{1,0:T(8,128)}, f32[8,9]{1,0:T(8,128)}, f32[3,8]{1,0:T(4,128)}) custom-call(bf16[4,8,2,2,8,8,128]{6,5,4,3,2,1,0:T(8,128)(2,1)} %bitcast.16, bf16[8,384]{1,0:T(8,128)(2,1)} %single_hbm.1, f32[8,9]{1,0:T(8,128)} %bitcast.24, f32[3,8]{1,0:T(4,128)} %translation_hbm.1, s32[8,128]{1,0:T(8,128)} %bitcast.25, s32[8,128]{1,0:T(8,128)} %bitcast.26, ...), custom_call_target="tpu_custom_call" | custom-call | tf_op jit(solution)/shard_map/structure_layers/pallas_call | solution.py:934
  84.0 1.7 %hand_over.1 = (f32[8,384]{1,0:T(8,128)}, f32[8,9]{1,0:T(8,128)}, f32[3,8]{1,0:T(4,128)}) custom-call(f32[8,384]{1,0:T(8,128)} %get-tuple-element.9.a, f32[8,9]{1,0:T(8,128)} %get-tuple-element.10.b, f32[3,8]{1,0:T(4,128)} %get-tuple-element.11.c), custom_call_target="tpu_custom_call" | custom-call | tf_op jit(solution)/shard_map/hand_over/pallas_call | solution.py:966

commit v5 on v4

--- a/solution.py
+++ b/solution.py
@@ -593,9 +593,9 @@
             n = far_step(t)
             if layer == 0:
 
-                @pl.when((t >= 2) & (t + 4 < nb))
+                @pl.when((t == 1) & (t + 6 < nb))
                 def _():
-                    exchange(t + 4, across)
+                    exchange(t + 6, across)
 
                 logits = scores[chunk_rows(n), :]
                 with jax.named_scope("tile_wait"):
@@ -771,12 +771,13 @@
     for layer in range(LAYERS):
         if layer == 0:
             exchange_across(2)
+            exchange_across(3)
         with jax.named_scope(f"key_wait_{layer}"):
             pltpu.make_async_copy(
                 kx.at[layer, 0 : g_count - 1], kx.at[layer, 0 : g_count - 1], kx_recv.at[layer]
             ).wait()
         if layer == 0:
-            exchange_across(3)
+            exchange_across(4)
         with jax.named_scope(f"key_{layer}"):
             key_phase(layer)
         with jax.named_scope(f"query_wait_{layer}"):
@@ -786,10 +787,10 @@
         with jax.named_scope(f"query_{layer}"):
             query_phase(layer)
         if layer == 0:
-            exchange_across(4)
+            exchange_across(5)
             with jax.named_scope(f"score_{layer}"):
                 score_phase()
-            exchange_across(5)
+            exchange_across(6)
         with jax.named_scope(f"chunk_{layer}"):
             chunk_phase(layer)
         with jax.named_scope(f"combine_{layer}"):

time: 87.1 us -> 87.8 us (level); the launches traced: 85.7 us -> 87.6 us
  Pallas kernels: 85 us -> 87 us
    pallas_call x1, Pallas kernels: 83.3 us -> 85.3 us  [on_device(): pl.pallas_call(functools.partial(kernel, (nx, nb, cores, rows, heads)), n...]
where the time goes in v5:
time: 87.8 us; the launch traced here: 87.6 us
  Pallas kernels  87 us (99%)
    pallas_call x1, Pallas kernels, on_device(): pl.pallas_call(functools.partial(kernel, (nx, nb, cores, rows, heads)), n...  85.3 us

profile of v5, /device:TPU:33, one launch (start us, length us, event | category | flops | bytes accessed | tf_op | source)
XLA Modules:
  0.0 87.6 jit_solution(5611482093347652210)
XLA Ops:
  0.6 85.3 %structure_layers.1 = (f32[8,384]{1,0:T(8,128)}, f32[8,9]{1,0:T(8,128)}, f32[3,8]{1,0:T(4,128)}) custom-call(bf16[4,8,2,2,8,8,128]{6,5,4,3,2,1,0:T(8,128)(2,1)} %bitcast.16, bf16[8,384]{1,0:T(8,128)(2,1)} %single_hbm.1, f32[8,9]{1,0:T(8,128)} %bitcast.24, f32[3,8]{1,0:T(4,128)} %translation_hbm.1, s32[8,128]{1,0:T(8,128)} %bitcast.25, s32[8,128]{1,0:T(8,128)} %bitcast.26, ...), custom_call_target="tpu_custom_call" | custom-call | tf_op jit(solution)/shard_map/structure_layers/pallas_call | solution.py:935
  86.0 1.7 %hand_over.1 = (f32[8,384]{1,0:T(8,128)}, f32[8,9]{1,0:T(8,128)}, f32[3,8]{1,0:T(4,128)}) custom-call(f32[8,384]{1,0:T(8,128)} %get-tuple-element.9.a, f32[8,9]{1,0:T(8,128)} %get-tuple-element.10.b, f32[3,8]{1,0:T(4,128)} %get-tuple-element.11.c), custom_call_target="tpu_custom_call" | custom-call | tf_op jit(solution)/shard_map/hand_over/pallas_call | solution.py:967
